TPU v7x, 8 devices: a whole 2x2x1 slice. The times are simulated.
8 devices in a mesh: rep: 1 (over z), mp: 2 (over y), tb: 2 (over x), ta: 2 (over core).
Axes of the slice: x: 2, y: 2, z: 1, core: 2. Of those that a mesh axis runs over, the one named last changes fastest.
Arguments:
- x_in: bfloat16 [4096, 4096], P(('rep', 'tb', 'ta'), 'mp')
- seg_ids: int32 [4096], P(('rep', 'tb', 'ta'))
- pos_ids: int32 [4096], P(('rep', 'tb', 'ta'))
- w_q: bfloat16 [2, 4096, 4096], P(None, ('tb', 'ta'), 'mp')
- w_k: bfloat16 [2, 4096, 128], P(None, ('tb', 'ta'))
- w_v: bfloat16 [2, 4096, 128], P(None, ('tb', 'ta'))
- w_gate: bfloat16 [2, 4096, 16384], P(None, ('tb', 'ta'), 'mp')
- w_up: bfloat16 [2, 4096, 16384], P(None, ('tb', 'ta'), 'mp')
- w_out: bfloat16 [2, 4096, 4096], P(None, 'mp', ('tb', 'ta'))
- w_down: bfloat16 [2, 16384, 4096], P(None, 'mp', ('tb', 'ta'))
- norm_gain: bfloat16 [2, 4096], replicated
Outputs:
- output: float32 [4096, 4096], P(('rep', 'tb', 'ta'), 'mp')
All inputs are finite; a program needn't handle non-finite values.
Results may differ from a plain program's by a relative error of at most 0.00501459.
Values are sent between devices in bfloat16 or wider.
A program may use at most 1 GiB of HBM per device.

v0:
```python
import jax
import jax.numpy as jnp
from jax import lax
from jax.sharding import PartitionSpec as P

ROPE_BASE = 10000.0
NORM_EPS = 1e-6
TOKEN_AXES = ("rep", "tb", "ta")
PLANE_AXES = ("tb", "ta")


def rope_tables(pos_ids, head_dim):
    half_dim = head_dim // 2
    inv_freq = ROPE_BASE ** (-(jnp.arange(half_dim, dtype=jnp.float32) * 2.0) / head_dim)
    angles = pos_ids.astype(jnp.float32)[:, None] * inv_freq[None, :]
    return jnp.cos(angles), jnp.sin(angles)


def apply_rope(rot_in, cos_tab, sin_tab):
    half_dim = rot_in.shape[-1] // 2
    lower_half = rot_in[..., :half_dim].astype(jnp.float32)
    upper_half = rot_in[..., half_dim:].astype(jnp.float32)
    return jnp.concatenate([lower_half * cos_tab - upper_half * sin_tab, upper_half * cos_tab + lower_half * sin_tab], axis=-1).astype(jnp.bfloat16)


def block_attention(q_rot, k_rot, v_proj, seg_q, pos_q, seg_k, pos_k):
    score_scale = q_rot.shape[-1] ** -0.5
    scores = jnp.einsum("thd,sd->hts", q_rot, k_rot, preferred_element_type=jnp.float32) * score_scale
    allowed = (seg_q[:, None] == seg_k[None, :]) & (pos_k[None, :] <= pos_q[:, None])
    scores = jnp.where(allowed[None], scores, -1e30)
    row_peak = jnp.max(scores, axis=-1, keepdims=True)
    exp_scores = jnp.exp(scores - row_peak)
    prob_bf16 = (exp_scores / jnp.sum(exp_scores, axis=-1, keepdims=True)).astype(jnp.bfloat16)
    return jnp.einsum("hts,sd->thd", prob_bf16, v_proj, preferred_element_type=jnp.float32).astype(jnp.bfloat16)


def solution(mesh):
    mp_size = mesh.shape["mp"]

    def device_body(x_loc, seg_ids, pos_ids, w_q, w_k, w_v, w_gate, w_up, w_out, w_down, gain_loc):
        num_tokens, embed_loc = x_loc.shape
        head_dim = w_k.shape[-1]
        width_q = w_q.shape[-1]
        width_ff = w_gate.shape[-1]
        edge_k = width_q + head_dim
        edge_v = edge_k + head_dim
        edge_g = edge_v + width_ff
        cos_tab, sin_tab = rope_tables(pos_ids, head_dim)
        hidden = x_loc.astype(jnp.float32)
        for layer_idx in range(w_q.shape[0]):
            sq_part = jnp.sum(hidden * hidden, axis=-1, keepdims=True)
            mean_sq = lax.psum(sq_part, "mp") / (embed_loc * mp_size)
            normed_loc = (hidden * lax.rsqrt(mean_sq + NORM_EPS) * gain_loc[layer_idx].astype(jnp.float32)).astype(jnp.bfloat16)
            normed = lax.all_gather(normed_loc, "mp", axis=1, tiled=True)
            w_in_loc = jnp.concatenate([w_q[layer_idx], w_k[layer_idx], w_v[layer_idx], w_gate[layer_idx], w_up[layer_idx]], axis=1)
            w_in = lax.all_gather(w_in_loc, PLANE_AXES, axis=0, tiled=True)
            proj_all = jnp.dot(normed, w_in, preferred_element_type=jnp.float32).astype(jnp.bfloat16)
            q_rot = apply_rope(proj_all[:, :width_q].reshape(num_tokens, width_q // head_dim, head_dim), cos_tab[:, None, :], sin_tab[:, None, :])
            k_rot = apply_rope(proj_all[:, width_q:edge_k], cos_tab, sin_tab)
            attn = block_attention(q_rot, k_rot, proj_all[:, edge_k:edge_v], seg_ids, pos_ids, seg_ids, pos_ids)
            mlp_act = (jax.nn.silu(proj_all[:, edge_v:edge_g].astype(jnp.float32)) * proj_all[:, edge_g:].astype(jnp.float32)).astype(jnp.bfloat16)
            w_back_loc = jnp.concatenate([w_out[layer_idx], w_down[layer_idx]], axis=0)
            w_back = lax.all_gather(w_back_loc, PLANE_AXES, axis=1, tiled=True)
            mixed = jnp.concatenate([attn.reshape(num_tokens, width_q), mlp_act], axis=1)
            part_sum = jnp.dot(mixed, w_back, preferred_element_type=jnp.float32)
            hidden = hidden + lax.psum_scatter(part_sum, "mp", scatter_dimension=1, tiled=True)
        return hidden

    col_spec = P(None, PLANE_AXES, "mp")
    kv_spec = P(None, PLANE_AXES, None)
    row_spec = P(None, "mp", PLANE_AXES)
    return jax.shard_map(
        device_body,
        mesh=mesh,
        in_specs=(P(TOKEN_AXES, "mp"), P(TOKEN_AXES), P(TOKEN_AXES), col_spec, kv_spec, kv_spec, col_spec, col_spec, row_spec, row_spec, P(None, "mp")),
        out_specs=P(TOKEN_AXES, "mp"),
        check_vma=False,
    )
```

profile of v0, /device:TPU:0, one launch (start us, length us, event | category | flops | bytes accessed | tf_op | source)
XLA Modules:
  0.0 3554.9 jit_solution(14265121517040771250)
XLA Ops:
  32.5 26.7 bitcast_dynamic-update-slice_fusion.1
  64.5 11.2 bitcast_dynamic-update-slice_fusion
  81.0 18.0 slice_bitcast_fusion.1
  99.0 30.1 pad_maximum_fusion
  132.8 876.6 %all-gather.9.cloned.1.call-done = bf16[4096,18688]{1,0:T(8,128)(2,1)} async-done(((bf16[1024,18688]{1,0:T(8,128)(2,1)}), bf16[4096,18688]{1,0:T(8,128)(2,1)}) %all-gather.9.cloned.1.call-update) | async-done | bytes 153092112 | tf_op jit(solution)/shard_map/all_gather | solution.py:56
  1009.4 172.4 %convolution_convert_fusion.1 = bf16[1024,18688]{1,0:T(8,128)(2,1)} fusion(bf16[1024,4096]{1,0:T(8,128)(2,1)} %all-gather.7.cloned.1.call-done, bf16[4096,18688]{1,0:T(8,128)(2,1)} %all-gather.9.cloned.1.call-done), kind=kOutput, calls=%fused_computation.15 | convolution fusion | flops 156785442816 | bytes 199753728 | tf_op jit(solution)/shard_map/dot_general | solution.py:57
  1196.9 31.2 fusion.82
  1228.1 23.8 fusion.47
  1258.4 21.0 fusion.17
  1279.4 216.4 %all-gather.11.cloned.1.call-done = bf16[10240,4096]{1,0:T(8,128)(2,1)} async-done(((bf16[10240,1024]{1,0:T(8,128)(2,1)}), bf16[10240,4096]{1,0:T(8,128)(2,1)}) %all-gather.11.cloned.1.call-update) | async-done | bytes 83886096 | tf_op jit(solution)/shard_map/all_gather | solution.py:63
  1495.8 97.3 %fusion.22 = f32[1024,4096]{1,0:T(8,128)} fusion(bf16[10240,4096]{1,0:T(8,128)(2,1)} %all-gather.11.cloned.1.call-done, bf16[1024,8192]{1,0:T(8,128)(2,1)} %fusion.17, bf16[1024,2048]{1,0:T(8,128)(2,1)} %copy.37), kind=kOutput, calls=%fused_computation.34 | convolution fusion | flops 85941288960 | bytes 121634816 | tf_op jit(solution)/shard_map/dot_general | solution.py:65
  1593.8 185.9 %reduce-scatter.3.cloned.1.call-done = f32[1024,2048]{1,0:T(8,128)} async-done(((f32[1024,4096]{1,0:T(8,128)}), f32[1024,2048]{1,0:T(8,128)}) %reduce-scatter.3.cloned.1.call-update) | async-done | bytes 8388624 | tf_op jit(solution)/shard_map/reduce_scatter | solution.py:66
  1790.4 6.8 multiply_convert_fusion
  1797.2 22.4 pad_maximum_fusion.1
  1819.8 840.7 %all-gather.15.cloned.1.call-done = bf16[4096,18688]{1,0:T(8,128)(2,1)} async-done(((bf16[1024,18688]{1,0:T(8,128)(2,1)}), bf16[4096,18688]{1,0:T(8,128)(2,1)}) %all-gather.15.cloned.1.call-update) | async-done | bytes 153092112 | tf_op jit(solution)/shard_map/all_gather | solution.py:56
  2660.4 103.7 %all-gather.13.cloned.1.call-done = bf16[1024,4096]{1,0:T(8,128)(2,1)} async-done(((bf16[1024,2048]{1,0:T(8,128)(2,1)}), bf16[1024,4096]{1,0:T(8,128)(2,1)}) %all-gather.13.cloned.1.call-update) | async-done | bytes 8388624 | tf_op jit(solution)/shard_map/all_gather | solution.py:54
  2764.1 172.5 %convolution_convert_fusion = bf16[1024,18688]{1,0:T(8,128)(2,1)} fusion(bf16[1024,4096]{1,0:T(8,128)(2,1)} %all-gather.13.cloned.1.call-done, bf16[4096,18688]{1,0:T(8,128)(2,1)} %all-gather.15.cloned.1.call-done), kind=kOutput, calls=%fused_computation.14 | convolution fusion | flops 156785442816 | bytes 199753728 | tf_op jit(solution)/shard_map/dot_general | solution.py:57
  2951.7 31.1 fusion.83
  2982.8 23.8 fusion.46
  3013.1 21.1 fusion.16
  3034.2 216.3 %all-gather.17.cloned.1.call-done = bf16[10240,4096]{1,0:T(8,128)(2,1)} async-done(((bf16[10240,1024]{1,0:T(8,128)(2,1)}), bf16[10240,4096]{1,0:T(8,128)(2,1)}) %all-gather.17.cloned.1.call-update) | async-done | bytes 83886096 | tf_op jit(solution)/shard_map/all_gather | solution.py:63
  3250.5 97.1 %fusion.26 = f32[1024,4096]{1,0:T(8,128)} fusion(bf16[10240,4096]{1,0:T(8,128)(2,1)} %all-gather.17.cloned.1.call-done, bf16[1024,8192]{1,0:T(8,128)(2,1)} %fusion.16, bf16[1024,2048]{1,0:T(8,128)(2,1)} %copy.39), kind=kOutput, calls=%fused_computation.39 | convolution fusion | flops 85941288960 | bytes 121634816 | tf_op jit(solution)/shard_map/dot_general | solution.py:65
  3347.6 186.5 %reduce-scatter.5.cloned.1.call-done = f32[1024,2048]{1,0:T(8,128)} async-done(((f32[1024,4096]{1,0:T(8,128)}), f32[1024,2048]{1,0:T(8,128)}) %reduce-scatter.5.cloned.1.call-update) | async-done | bytes 8388624 | tf_op jit(solution)/shard_map/reduce_scatter | solution.py:66
  3534.1 13.5 fusion.45
  (92 shorter events, 94.0 us)
Async XLA Ops:
  6.5 126.3 %all-gather.7.cloned.1.call-start = ((), (), s32[]{:S(2)}) async-start(), calls=%async_computation.2 | async-start | bytes 12582912 | tf_op jit(solution)/shard_map/all_gather | solution.py:54
  8.4 22.3 copy-start.6
  8.4 23.2 copy-start.7
  24.6 984.9 %all-gather.9.cloned.1.call-start = ((), (), s32[]{:S(2)}) async-start(), calls=%async_computation.3 | async-start | bytes 191365120 | tf_op jit(solution)/shard_map/all_gather | solution.py:56
  32.5 26.8 slice-start
  32.5 26.8 slice-start.1
  32.5 26.8 slice-start.2
  32.5 26.8 slice-start.3
  32.5 28.4 slice-start.4
  32.5 29.6 slice-start.5
  32.5 30.7 slice-start.6
  32.5 31.9 slice-start.7
  75.7 1420.1 %all-gather.11.cloned.1.call-start = ((), (), s32[]{:S(2)}) async-start(), calls=%async_computation.4 | async-start | bytes 104857600 | tf_op jit(solution)/shard_map/all_gather | solution.py:63
  129.1 1650.6 %reduce-scatter.3.cloned.1.call-start = ((), (), s32[]{:S(2)}) async-start(), calls=%async_computation.5 | async-start | bytes 25165824 | tf_op jit(solution)/shard_map/reduce_scatter | solution.py:66
  1189.5 7.4 copy-start
  1189.5 7.4 copy-start.2
  1189.5 7.4 copy-start.4
  1593.2 1067.2 %all-gather.15.cloned.1.call-start = ((), (), s32[]{:S(2)}) async-start(), calls=%async_computation.7 | async-start | bytes 191365120 | tf_op jit(solution)/shard_map/all_gather | solution.py:56
  1593.2 197.1 %copy-start.11 = (f32[1,2048]{1,0:T(1,128)S(1)}, f32[1,2048]{1,0:T(1,128)}, u32[]{:S(2)}) copy-start(f32[1,2048]{1,0:T(1,128)} %get-tuple-element.32) | copy-start | bytes 24580
  1593.8 1170.3 %all-gather.13.cloned.1.call-start = ((), (), s32[]{:S(2)}) async-start(), calls=%async_computation.6 | async-start | bytes 12582912 | tf_op jit(solution)/shard_map/all_gather | solution.py:54
  1797.2 1453.3 %all-gather.17.cloned.1.call-start = ((), (), s32[]{:S(2)}) async-start(), calls=%async_computation.8 | async-start | bytes 104857600 | tf_op jit(solution)/shard_map/all_gather | solution.py:63
  1819.7 1714.4 %reduce-scatter.5.cloned.1.call-start = ((), (), s32[]{:S(2)}) async-start(), calls=%async_computation.9 | async-start | bytes 25165824 | tf_op jit(solution)/shard_map/reduce_scatter | solution.py:66
  2936.6 9.7 copy-start.1
  2936.6 9.7 copy-start.3
  (7 other events, 25.8 us)
Sparse Core Ops, SparseCore 0:
  24.7 103.7 all-gather.6
  130.0 879.3 all-gather.8
  1011.0 484.8 all-gather.10
  1593.3 186.3 reduce-scatter.2
  1781.1 879.3 all-gather.14
  2661.8 102.2 all-gather.12
  2765.6 484.8 all-gather.16
  3347.8 186.2 reduce-scatter.4
where the time goes:
time: 3560 us; the launch traced here: 3550 us
  waiting for transfers between devices  2630 us (74%)
  matrix products  649 us (18%)
  other arithmetic  152 us (4%)
  local copies, waits for them, and re-layouts  101 us (3%)
    all_gather x2, waiting for transfers between devices, device_body(): w_in = lax.all_gather(w_in_loc, PLANE_AXES, axis=0, tiled=True)  1720 us
    all_gather x2, waiting for transfers between devices, device_body(): w_back = lax.all_gather(w_back_loc, PLANE_AXES, axis=1, tiled=True)  433 us
    reduce_scatter x2, waiting for transfers between devices, device_body(): lax.psum_scatter(part_sum, 'mp', scatter_dimension=1, tiled=True)  372 us
    dot_general x2, matrix products, device_body(): jnp.dot(normed, w_in, preferred_element_type=jnp.float32)  345 us
    dot_general x2, matrix products, device_body(): part_sum = jnp.dot(mixed, w_back, preferred_element_type=jnp.float32)  194 us
    all_gather x2, waiting for transfers between devices, device_body(): normed = lax.all_gather(normed_loc, 'mp', axis=1, tiled=True)  104 us
  transfers between devices with their start and end apart: 8, of which 7 were waited for; matrix products, arithmetic and copies ran while one was open for 19% of the time, Pallas kernels for 0%

commit v1 on v0

v1 whole, which is shorter than its diff:
```python
import functools

import jax
import jax.numpy as jnp
from jax import lax
from jax.experimental import pallas as pl
from jax.experimental.pallas import tpu as pltpu
from jax.sharding import PartitionSpec as P


ROPE_BASE = 10000.0
NORM_EPS = 1e-6
TOKEN_AXES = ("rep", "tb", "ta")
PLANE_AXES = ("tb", "ta")
SWAP = ((0, 1), (1, 0))
CHUNKS = 4
VMEM_LIMIT = 60 * 1024 * 1024


def rope_tables(pos_ids, head_dim):
    half_dim = head_dim // 2
    inv_freq = ROPE_BASE ** (-(jnp.arange(half_dim, dtype=jnp.float32) * 2.0) / head_dim)
    angles = pos_ids.astype(jnp.float32)[:, None] * inv_freq[None, :]
    return jnp.cos(angles), jnp.sin(angles)


def apply_rope(rot_in, cos_tab, sin_tab):
    half_dim = rot_in.shape[-1] // 2
    lower_half = rot_in[..., :half_dim].astype(jnp.float32)
    upper_half = rot_in[..., half_dim:].astype(jnp.float32)
    return jnp.concatenate([lower_half * cos_tab - upper_half * sin_tab, upper_half * cos_tab + lower_half * sin_tab], axis=-1).astype(jnp.bfloat16)


def block_attention(q_rot, k_rot, v_proj, seg, pos):
    score_scale = q_rot.shape[-1] ** -0.5
    scores = jnp.einsum("thd,sd->hts", q_rot, k_rot, preferred_element_type=jnp.float32) * score_scale
    allowed = (seg[:, None] == seg[None, :]) & (pos[None, :] <= pos[:, None])
    scores = jnp.where(allowed[None], scores, -1e30)
    row_peak = jnp.max(scores, axis=-1, keepdims=True)
    exp_scores = jnp.exp(scores - row_peak)
    prob_bf16 = (exp_scores / jnp.sum(exp_scores, axis=-1, keepdims=True)).astype(jnp.bfloat16)
    return jnp.einsum("hts,sd->thd", prob_bf16, v_proj, preferred_element_type=jnp.float32).astype(jnp.bfloat16)


def hop(val, axis):
    return lax.ppermute(val, axis, SWAP)


def dot32(a, b):
    return jnp.dot(a, b, preferred_element_type=jnp.float32)


def in_kernel(gated, idx_ref, *refs):
    h_refs, refs, out_ref = refs[0:4], refs[4:-1], refs[-1]
    rows = h_refs[0].shape[1]
    for block in range(2):
        sl = slice(block * rows, (block + 1) * rows)

        def product(pieces):
            total = None
            for h_ref, piece in zip(h_refs, pieces):
                term = dot32(h_ref[block], piece[...])
                total = term if total is None else total + term
            return total.astype(jnp.bfloat16)

        if gated:
            gate = product(refs[0:4]).astype(jnp.float32)
            up = product(refs[4:8]).astype(jnp.float32)
            out_ref[sl, :] = (jax.nn.silu(gate) * up).astype(jnp.bfloat16)
        else:
            out_ref[sl, :] = product(refs[0:4])


def in_proj(idx, h, pieces, maps, n_cols, gated, tile=256):
    _, blocks, block_tok, half = h.shape
    tokens, width, depth = blocks * block_tok, 2 * half, half // 2
    once = dict(pipeline_mode=pl.Buffered(1))
    h_block = (None, blocks, block_tok, depth)
    specs = [
        pl.BlockSpec(h_block, lambda i, s: (1 - s[1], 0, 0, s[2]), **once),
        pl.BlockSpec(h_block, lambda i, s: (1 - s[1], 0, 0, 1 - s[2]), **once),
        pl.BlockSpec(h_block, lambda i, s: (s[1], 0, 0, s[2]), **once),
        pl.BlockSpec(h_block, lambda i, s: (s[1], 0, 0, 1 - s[2]), **once),
    ]
    for piece, fn in zip(pieces, maps):
        if piece.ndim == 3:
            layer, col = fn
            specs.append(pl.BlockSpec((None, depth, tile), functools.partial(lambda i, s, layer, col: (layer, 0, col(i, s)), layer=layer, col=col)))
        else:
            specs.append(pl.BlockSpec((depth, tile), functools.partial(lambda i, s, col: (0, col(i, s)), col=fn)))
    flops = 2 * tokens * width * n_cols * (2 if gated else 1)
    return pl.pallas_call(
        functools.partial(in_kernel, gated),
        grid_spec=pltpu.PrefetchScalarGridSpec(
            num_scalar_prefetch=1,
            grid=(n_cols // tile,),
            in_specs=specs,
            out_specs=pl.BlockSpec((tokens, tile), lambda i, s: (0, i)),
        ),
        out_shape=jax.ShapeDtypeStruct((tokens, n_cols), jnp.bfloat16),
        compiler_params=pltpu.CompilerParams(vmem_limit_bytes=VMEM_LIMIT),
        cost_estimate=pl.CostEstimate(flops=flops, bytes_accessed=flops // 1000, transcendentals=0),
    )(idx, h, h, h, h, *pieces)


def back_kernel(idx_ref, *refs):
    acts, weights, (send_ref, keep_ref) = refs[0:5], refs[5:13], refs[13:15]
    width = weights[0].shape[-1]
    depth = acts[0].shape[1]

    def product(wo, wd):
        total = dot32(acts[0][...], wo[...])
        for j in range(4):
            total = total + dot32(acts[1 + j][...], wd[j * depth:(j + 1) * depth, :])
        return total

    same = idx_ref[1] == 1
    first = [product(weights[0], weights[1]), product(weights[2], weights[3])]
    second = [product(weights[4], weights[5]), product(weights[6], weights[7])]

    @pl.when(same)
    def _():
        for p in range(2):
            send_ref[:, p * width:(p + 1) * width] = second[p]
            keep_ref[:, p * width:(p + 1) * width] = first[p]

    @pl.when(jnp.logical_not(same))
    def _():
        for p in range(2):
            send_ref[:, p * width:(p + 1) * width] = first[p]
            keep_ref[:, p * width:(p + 1) * width] = second[p]


def back_proj(idx, acts, w_out, w_down, own_p, recv, recv_p, layer, w, rows=256):
    tokens, depth = acts[0].shape
    width = recv[1].shape[1]
    once = dict(pipeline_mode=pl.Buffered(1))
    specs = [pl.BlockSpec((rows, depth), lambda i, s: (i, 0)) for _ in acts]
    specs.append(pl.BlockSpec((None, depth, width), lambda i, s: (layer, s[0], w), **once))
    specs.append(pl.BlockSpec((None, 4 * depth, width), lambda i, s: (layer, s[0], w), **once))
    specs.append(pl.BlockSpec((depth, width), lambda i, s: (0, w), **once))
    specs.append(pl.BlockSpec((4 * depth, width), lambda i, s: (0, w), **once))
    for _ in range(2):
        specs.append(pl.BlockSpec((depth, width), lambda i, s: (0, w), **once))
        specs.append(pl.BlockSpec((4 * depth, width), lambda i, s: (0, 0), **once))
    flops = 2 * tokens * 5 * depth * 4 * width
    out = jax.ShapeDtypeStruct((tokens, 2 * width), jnp.float32)
    return pl.pallas_call(
        back_kernel,
        grid_spec=pltpu.PrefetchScalarGridSpec(
            num_scalar_prefetch=1,
            grid=(tokens // rows,),
            in_specs=specs,
            out_specs=[pl.BlockSpec((rows, 2 * width), lambda i, s: (i, 0))] * 2,
        ),
        out_shape=[out, out],
        compiler_params=pltpu.CompilerParams(vmem_limit_bytes=VMEM_LIMIT),
        cost_estimate=pl.CostEstimate(flops=flops, bytes_accessed=flops // 1000, transcendentals=0),
    )(idx, *acts, w_out, w_down, *own_p, *recv, *recv_p)


def solution(mesh):
    def device_body(x_loc, seg_ids, pos_ids, w_q, w_k, w_v, w_gate, w_up, w_out, w_down, gain):
        tb = lax.axis_index("tb")
        ta = lax.axis_index("ta")
        mp = lax.axis_index("mp")
        num_tok, half = x_loc.shape
        quarter = half // 2
        layers = w_q.shape[0]
        head_dim = w_k.shape[-1]
        nq = w_q.shape[-1] // 2
        nf = w_gate.shape[-1] // 2
        cin = nf // CHUNKS
        cbk = w_out.shape[-1] // CHUNKS
        idx = jnp.stack([tb, (tb == mp).astype(jnp.int32), ta]).astype(jnp.int32)

        def part(w, l, r0, nr, c0, nc):
            return lax.dynamic_slice(w, (l, r0, c0), (1, nr, nc))[0]

        def gather_rows(v):
            vy = hop(v, "mp")
            vx = hop(v, "tb")
            vxy = hop(vx, "mp")
            return [[v, vx], [vy, vxy]]

        def gain_half(l, side):
            return lax.dynamic_slice_in_dim(gain[l], side * half, half).astype(jnp.float32)

        ids = jnp.stack([seg_ids, pos_ids])
        ids_f = hop(ids, "tb")
        segs, poss = (ids[0], ids_f[0]), (ids[1], ids_f[1])
        cos_tab, sin_tab = rope_tables(jnp.concatenate(poss), head_dim)
        hidden = x_loc.astype(jnp.float32)
        kv_own = jnp.concatenate([w for l in range(layers) for w in (w_k[l], w_v[l])], axis=1)
        kv_recv = hop(kv_own, "tb")
        kv_p = hop(kv_own, "ta")
        kv_e = hop(kv_recv, "ta")
        for l in range(layers):
            q_p = hop(part(w_q, l, 0, quarter, tb * nq, nq), "ta")
            g_p = hop(part(w_gate, l, 0, quarter, tb * nf, nf), "ta")
            u_p = hop(part(w_up, l, 0, quarter, tb * nf, nf), "ta")
            o_p = hop(part(w_out, l, tb * nq, nq, 0, quarter), "ta")
            d_p = hop(part(w_down, l, tb * nf, nf, 0, quarter), "ta")
            q_x = hop(part(w_q, l, 0, quarter, (1 - tb) * nq, nq), "tb")
            g_x = [hop(part(w_gate, l, 0, quarter, (1 - tb) * nf + j * cin, cin), "tb") for j in range(CHUNKS)]
            u_x = [hop(part(w_up, l, 0, quarter, (1 - tb) * nf + j * cin, cin), "tb") for j in range(CHUNKS)]
            o_x = hop(part(w_out, l, (1 - tb) * nq, nq, 0, quarter), "tb")
            d_x = [hop(part(w_down, l, (1 - tb) * nf, nf, w * cbk, cbk), "tb") for w in range(CHUNKS)]
            q_e = hop(q_x, "ta")
            g_e = [hop(g_x[j], "ta") for j in range(CHUNKS)]
            u_e = [hop(u_x[j], "ta") for j in range(CHUNKS)]
            o_e = hop(o_x, "ta")
            d_e = [hop(d_x[w], "ta") for w in range(CHUNKS)]

            if l == 0:
                full = [[v.astype(jnp.float32) for v in side] for side in gather_rows(x_loc)]
                scale = [lax.rsqrt(sum(jnp.sum(side[t] * side[t], axis=-1, keepdims=True) for side in full) / (2 * half) + NORM_EPS) for t in range(2)]
                gains = [gain_half(l, mp), gain_half(l, 1 - mp)]
                sides = [[(full[k][t] * scale[t] * gains[k]).astype(jnp.bfloat16) for t in range(2)] for k in range(2)]
            else:
                mean_sq = lax.psum(jnp.sum(hidden * hidden, axis=-1, keepdims=True), "mp") / (2 * half)
                sides = gather_rows((hidden * lax.rsqrt(mean_sq + NORM_EPS) * gain_half(l, mp)).astype(jnp.bfloat16))
            h = jnp.concatenate([v for side in sides for v in side], axis=0).reshape(2, 2, num_tok, half)

            tile = 256
            qt, ct, ft = nq // tile, cin // tile, nf // tile
            step = lambda i, s: i
            q = in_proj(idx, h, [w_q, q_p, q_x, q_e], [(l, lambda i, s: s[0] * qt + i), step, step, step], nq, False)
            kv = in_proj(idx, h, [kv_own, kv_p, kv_recv, kv_e], [lambda i, s, l=l: l] * 4, tile, False)
            q_rot = apply_rope(q.reshape(2 * num_tok, nq // head_dim, head_dim), cos_tab[:, None, :], sin_tab[:, None, :])
            k_rot = apply_rope(kv[:, :head_dim], cos_tab, sin_tab)
            v_proj = kv[:, head_dim:]
            blocks = []
            for t in range(2):
                sl = slice(t * num_tok, (t + 1) * num_tok)
                blocks.append(block_attention(q_rot[sl], k_rot[sl], v_proj[sl], segs[t], poss[t]).reshape(num_tok, nq))
            acts = [jnp.concatenate(blocks, axis=0)]
            for j in range(CHUNKS):
                own_map = (l, functools.partial(lambda i, s, j: s[0] * ft + j * ct + i, j=j))
                p_map = functools.partial(lambda i, s, j: j * ct + i, j=j)
                acts.append(in_proj(
                    idx, h, [w_gate, g_p, g_x[j], g_e[j], w_up, u_p, u_x[j], u_e[j]],
                    [own_map, p_map, step, step] * 2, cin, True))
            parts_a, parts_b = [], []
            for w in range(CHUNKS):
                send, keep = back_proj(idx, acts, w_out, w_down, (o_p, d_p), (o_x, d_x[w]), (o_e, d_e[w]), l, w)
                if w < CHUNKS - 1:
                    summed = keep + hop(send, "mp")
                    d = summed[:num_tok] + hop(summed[num_tok:], "tb")
                else:
                    passed = send[:num_tok] + hop(send[num_tok:], "tb")
                    kept = keep[:num_tok] + hop(keep[num_tok:], "tb")
                    d = kept + hop(passed, "mp")
                parts_a.append(d[:, :cbk])
                parts_b.append(d[:, cbk:])
            first = ta == 0
            pa = jnp.concatenate(parts_a, axis=1)
            pb = jnp.concatenate(parts_b, axis=1)
            hidden = hidden + jnp.concatenate([jnp.where(first, pa, pb), jnp.where(first, pb, pa)], axis=1)
        return hidden

    col_spec = P(None, PLANE_AXES, "mp")
    kv_spec = P(None, PLANE_AXES, None)
    row_spec = P(None, "mp", PLANE_AXES)
    return jax.shard_map(
        device_body,
        mesh=mesh,
        in_specs=(P(TOKEN_AXES, "mp"), P(TOKEN_AXES), P(TOKEN_AXES), col_spec, kv_spec, kv_spec, col_spec, col_spec, row_spec, row_spec, P(None, None)),
        out_specs=P(TOKEN_AXES, "mp"),
        check_vma=False,
    )
```

time: 3560 us -> 2250 us (0.63)
  waiting for transfers between devices: 2630 us -> 1050 us
  Pallas kernels: 0 us -> 686 us
  matrix products: 649 us -> 135 us
  starting transfers between devices: 0.46 us -> 75.5 us
  local copies, waits for them, and re-layouts: 101 us -> 151 us
    all_gather x6 -> x0, waiting for transfers between devices: 2250 us -> none  [the longest x2 1720 us: device_body(): w_in = lax.all_gather(w_in_loc, PLANE_AXES, axis=0, tiled=True)]
    ppermute x0 -> x94, waiting for transfers between devices: none -> 1050 us  [hop(): return lax.ppermute(val, axis, SWAP)]
    pallas_call x0 -> x20, Pallas kernels: none -> 686 us  [the longest x12 439 us: in_proj(): pl.pallas_call(functools.partial(in_kernel, gated), grid_spec=pltpu.Prefe...]
    dot_general x4 -> x0, matrix products: 539 us -> none  [the longest x2 345 us: device_body(): jnp.dot(normed, w_in, preferred_element_type=jnp.float32)]
    reduce_scatter x2 -> x0, waiting for transfers between devices: 372 us -> none  [device_body(): lax.psum_scatter(part_sum, 'mp', scatter_dimension=1, tiled=True)]
    ppermute x0 -> x94, starting transfers between devices: none -> 75.5 us  [hop(): return lax.ppermute(val, axis, SWAP)]
    squeeze x2 -> x9, local copies, waits for them, and re-layouts: 23.3 us -> 81 us  [the longest x8 80.9 us: part(): return lax.dynamic_slice(w, (l, r0, c0), (1, nr, nc))[0]]
    convert_element_type x4 -> x2, other arithmetic: 54 us -> 16.1 us  [the longest x1 10 us: device_body(): (full[k][t] * scale[t] * gains[k]).astype(jnp.bfloat16)]
  transfers between devices with their start and end apart: 8 -> 94, of which waited for: 7 -> 28; matrix products, arithmetic and copies ran while one was open for 19% -> 17% of each run, Pallas kernels for 0% -> 31%
where the time goes in v1:
time: 2250 us; the launch traced here: 2240 us
  waiting for transfers between devices  1050 us (47%)
  Pallas kernels  686 us (30%)
  local copies, waits for them, and re-layouts  151 us (7%)
  matrix products  135 us (6%)
  other arithmetic  134 us (6%)
  starting transfers between devices  75.5 us (3%)
    ppermute x94, waiting for transfers between devices, hop(): return lax.ppermute(val, axis, SWAP)  1050 us
    pallas_call x12, Pallas kernels, in_proj(): pl.pallas_call(functools.partial(in_kernel, gated), grid_spec=pltpu.Prefe...  439 us
    pallas_call x8, Pallas kernels, back_proj(): pl.pallas_call(back_kernel, grid_spec=pltpu.PrefetchScalarGridSpec(num_sc...  247 us
    sub x4, matrix products, block_attention(): exp_scores = jnp.exp(scores - row_peak)  83.2 us
    squeeze x8, local copies, waits for them, and re-layouts, part(): return lax.dynamic_slice(w, (l, r0, c0), (1, nr, nc))[0]  80.9 us
    ppermute x94, starting transfers between devices, hop(): return lax.ppermute(val, axis, SWAP)  75.5 us
    dot_general x4, matrix products, block_attention(): jnp.einsum('hts,sd->thd', prob_bf16, v_proj, preferred_element_type=jnp.f...  51.5 us
  transfers between devices with their start and end apart: 94, of which 28 were waited for; matrix products, arithmetic and copies ran while one was open for 17% of the time, Pallas kernels for 31%

profile of v1, /device:TPU:0, one launch (start us, length us, event | category | flops | bytes accessed | tf_op | source)
XLA Modules:
  0.0 2237.6 jit_solution(9914795335933452982)
XLA Ops:
  396.9 45.1 %shard_map.111.refs_1_ = bf16[2048,1024]{1,0:T(8,128)(2,1)} custom-call(s32[3]{0:T(128)} %pad_add_fusion.1.idx_ref, bf16[2,2,1024,2048]{3,2,1,0:T(8,128)(2,1)} %bitcast.215, bf16[2,2,1024,2048]{3,2,1,0:T(8,128)(2,1)} %bitcast.213, bf16[2,2,1024,2048]{3,2,1,0:T(8,128)(2,1)} %bitcast.214, bf16[2,2,1024,2048]{3,2,1,0:T(8,128)(2,1)} %bitcast.212, ...), custom_call_target="tpu_custom_call" | custom-call | flops 34359738368 | bytes 34359736 | tf_op jit(solution)/shard_map/pallas_call | solution.py:92
  443.2 43.2 %collective-permute-done.24.refs_6_ = bf16[1024,1024]{1,0:T(8,128)(2,1)} collective-permute-done((bf16[1024,1024]{1,0:T(8,128)(2,1)}, bf16[1024,1024]{1,0:T(8,128)(2,1)}, u32[]{:S(2)}, u32[]{:S(2)}) %collective-permute-start.24) | collective-permute-done | bytes 2097184 | tf_op jit(solution)/shard_map/ppermute | solution.py:46
  486.4 44.9 %collective-permute-done.26.refs_10_ = bf16[1024,1024]{1,0:T(8,128)(2,1)} collective-permute-done((bf16[1024,1024]{1,0:T(8,128)(2,1)}, bf16[1024,1024]{1,0:T(8,128)(2,1)}, u32[]{:S(2)}, u32[]{:S(2)}) %collective-permute-start.26) | collective-permute-done | bytes 2097184 | tf_op jit(solution)/shard_map/ppermute | solution.py:46
  531.8 45.0 %shard_map.112.refs_2_ = bf16[2048,1024]{1,0:T(8,128)(2,1)} custom-call(s32[3]{0:T(128)} %pad_add_fusion.1.idx_ref, bf16[2,2,1024,2048]{3,2,1,0:T(8,128)(2,1)} %bitcast.216, bf16[2,2,1024,2048]{3,2,1,0:T(8,128)(2,1)} %bitcast.217, bf16[2,2,1024,2048]{3,2,1,0:T(8,128)(2,1)} %bitcast.218, bf16[2,2,1024,2048]{3,2,1,0:T(8,128)(2,1)} %bitcast.219, ...), custom_call_target="tpu_custom_call" | custom-call | flops 34359738368 | bytes 34359736 | tf_op jit(solution)/shard_map/pallas_call | solution.py:92
  579.4 45.4 %shard_map.113.refs_3_ = bf16[2048,1024]{1,0:T(8,128)(2,1)} custom-call(s32[3]{0:T(128)} %pad_add_fusion.1.idx_ref, bf16[2,2,1024,2048]{3,2,1,0:T(8,128)(2,1)} %bitcast.220, bf16[2,2,1024,2048]{3,2,1,0:T(8,128)(2,1)} %bitcast.221, bf16[2,2,1024,2048]{3,2,1,0:T(8,128)(2,1)} %bitcast.222, bf16[2,2,1024,2048]{3,2,1,0:T(8,128)(2,1)} %bitcast.223, ...), custom_call_target="tpu_custom_call" | custom-call | flops 34359738368 | bytes 34359736 | tf_op jit(solution)/shard_map/pallas_call | solution.py:92
  627.5 43.2 %collective-permute-done.36.refs_10_ = bf16[4096,256]{1,0:T(8,128)(2,1)} collective-permute-done((bf16[4096,256]{1,0:T(8,128)(2,1)}, bf16[4096,256]{1,0:T(8,128)(2,1)}, u32[]{:S(2)}, u32[]{:S(2)}) %collective-permute-start.36) | collective-permute-done | bytes 2097184 | tf_op jit(solution)/shard_map/ppermute | solution.py:46
  672.9 45.0 %shard_map.114.refs_4_ = bf16[2048,1024]{1,0:T(8,128)(2,1)} custom-call(s32[3]{0:T(128)} %pad_add_fusion.1.idx_ref, bf16[2,2,1024,2048]{3,2,1,0:T(8,128)(2,1)} %bitcast.224, bf16[2,2,1024,2048]{3,2,1,0:T(8,128)(2,1)} %bitcast.225, bf16[2,2,1024,2048]{3,2,1,0:T(8,128)(2,1)} %bitcast.226, bf16[2,2,1024,2048]{3,2,1,0:T(8,128)(2,1)} %bitcast.227, ...), custom_call_target="tpu_custom_call" | custom-call | flops 34359738368 | bytes 34359736 | tf_op jit(solution)/shard_map/pallas_call | solution.py:92
  917.1 58.1 %collective-permute-done.38 = f32[2048,512]{1,0:T(8,128)} collective-permute-done((f32[2048,512]{1,0:T(8,128)}, f32[2048,512]{1,0:T(8,128)}, u32[]{:S(2)}, u32[]{:S(2)}) %collective-permute-start.38) | collective-permute-done | bytes 4194336 | tf_op jit(solution)/shard_map/ppermute | solution.py:46
  982.9 82.1 %collective-permute-done.42 = f32[2048,512]{1,0:T(8,128)} collective-permute-done((f32[2048,512]{1,0:T(8,128)}, f32[2048,512]{1,0:T(8,128)}, u32[]{:S(2)}, u32[]{:S(2)}) %collective-permute-start.42) | collective-permute-done | bytes 4194336 | tf_op jit(solution)/shard_map/ppermute | solution.py:46
  1071.6 37.6 %collective-permute-done.48 = f32[1024,512]{1,0:T(8,128)} collective-permute-done((f32[1024,512]{1,0:T(8,128)S(1)}, f32[1024,512]{1,0:T(8,128)}, u32[]{:S(2)}, u32[]{:S(2)}) %collective-permute-start.48) | collective-permute-done | bytes 2097184 | tf_op jit(solution)/shard_map/ppermute | solution.py:46
  1138.7 87.5 %collective-permute-done.49 = bf16[1024,2048]{1,0:T(8,128)(2,1)S(1)} collective-permute-done((bf16[1024,2048]{1,0:T(8,128)(2,1)S(1)}, bf16[1024,2048]{1,0:T(8,128)(2,1)S(1)}, u32[]{:S(2)}, u32[]{:S(2)}) %collective-permute-start.49) | collective-permute-done | bytes 4194336 | tf_op jit(solution)/shard_map/ppermute | solution.py:46
  1229.2 43.0 %collective-permute-done.53.refs_6_ = bf16[1024,1024]{1,0:T(8,128)(2,1)S(1)} collective-permute-done((bf16[1024,1024]{1,0:T(8,128)(2,1)S(1)}, bf16[1024,1024]{1,0:T(8,128)(2,1)S(1)}, u32[]{:S(2)}, u32[]{:S(2)}) %collective-permute-start.53) | collective-permute-done | bytes 2097184 | tf_op jit(solution)/shard_map/ppermute | solution.py:46
  1274.2 43.1 %collective-permute-done.51 = bf16[1024,2048]{1,0:T(8,128)(2,1)S(1)} collective-permute-done((bf16[1024,2048]{1,0:T(8,128)(2,1)S(1)}, bf16[1024,2048]{1,0:T(8,128)(2,1)S(1)}, u32[]{:S(2)}, u32[]{:S(2)}) %collective-permute-start.51) | collective-permute-done | bytes 4194336 | tf_op jit(solution)/shard_map/ppermute | solution.py:46
  1504.3 45.3 %shard_map.121.refs_1_ = bf16[2048,1024]{1,0:T(8,128)(2,1)} custom-call(s32[3]{0:T(128)} %pad_add_fusion.1.idx_ref, bf16[2,2,1024,2048]{3,2,1,0:T(8,128)(2,1)} %bitcast.239, bf16[2,2,1024,2048]{3,2,1,0:T(8,128)(2,1)} %bitcast.237, bf16[2,2,1024,2048]{3,2,1,0:T(8,128)(2,1)} %bitcast.238, bf16[2,2,1024,2048]{3,2,1,0:T(8,128)(2,1)} %bitcast.236, ...), custom_call_target="tpu_custom_call" | custom-call | flops 34359738368 | bytes 34359736 | tf_op jit(solution)/shard_map/pallas_call | solution.py:92
  1550.5 43.5 %collective-permute-done.69.refs_6_ = bf16[1024,1024]{1,0:T(8,128)(2,1)} collective-permute-done((bf16[1024,1024]{1,0:T(8,128)(2,1)}, bf16[1024,1024]{1,0:T(8,128)(2,1)}, u32[]{:S(2)}, u32[]{:S(2)}) %collective-permute-start.69) | collective-permute-done | bytes 2097184 | tf_op jit(solution)/shard_map/ppermute | solution.py:46
  1594.1 44.9 %collective-permute-done.71.refs_10_ = bf16[1024,1024]{1,0:T(8,128)(2,1)} collective-permute-done((bf16[1024,1024]{1,0:T(8,128)(2,1)}, bf16[1024,1024]{1,0:T(8,128)(2,1)}, u32[]{:S(2)}, u32[]{:S(2)}) %collective-permute-start.71) | collective-permute-done | bytes 2097184 | tf_op jit(solution)/shard_map/ppermute | solution.py:46
  1639.6 45.0 %shard_map.122.refs_2_ = bf16[2048,1024]{1,0:T(8,128)(2,1)} custom-call(s32[3]{0:T(128)} %pad_add_fusion.1.idx_ref, bf16[2,2,1024,2048]{3,2,1,0:T(8,128)(2,1)} %bitcast.240, bf16[2,2,1024,2048]{3,2,1,0:T(8,128)(2,1)} %bitcast.241, bf16[2,2,1024,2048]{3,2,1,0:T(8,128)(2,1)} %bitcast.242, bf16[2,2,1024,2048]{3,2,1,0:T(8,128)(2,1)} %bitcast.243, ...), custom_call_target="tpu_custom_call" | custom-call | flops 34359738368 | bytes 34359736 | tf_op jit(solution)/shard_map/pallas_call | solution.py:92
  1687.1 45.1 %shard_map.123.refs_3_ = bf16[2048,1024]{1,0:T(8,128)(2,1)} custom-call(s32[3]{0:T(128)} %pad_add_fusion.1.idx_ref, bf16[2,2,1024,2048]{3,2,1,0:T(8,128)(2,1)} %bitcast.244, bf16[2,2,1024,2048]{3,2,1,0:T(8,128)(2,1)} %bitcast.245, bf16[2,2,1024,2048]{3,2,1,0:T(8,128)(2,1)} %bitcast.246, bf16[2,2,1024,2048]{3,2,1,0:T(8,128)(2,1)} %bitcast.247, ...), custom_call_target="tpu_custom_call" | custom-call | flops 34359738368 | bytes 34359736 | tf_op jit(solution)/shard_map/pallas_call | solution.py:92
  1734.8 43.5 %collective-permute-done.81.refs_10_ = bf16[4096,256]{1,0:T(8,128)(2,1)} collective-permute-done((bf16[4096,256]{1,0:T(8,128)(2,1)}, bf16[4096,256]{1,0:T(8,128)(2,1)}, u32[]{:S(2)}, u32[]{:S(2)}) %collective-permute-start.81) | collective-permute-done | bytes 2097184 | tf_op jit(solution)/shard_map/ppermute | solution.py:46
  1780.3 45.0 %shard_map.124.refs_4_ = bf16[2048,1024]{1,0:T(8,128)(2,1)} custom-call(s32[3]{0:T(128)} %pad_add_fusion.1.idx_ref, bf16[2,2,1024,2048]{3,2,1,0:T(8,128)(2,1)} %bitcast.248, bf16[2,2,1024,2048]{3,2,1,0:T(8,128)(2,1)} %bitcast.249, bf16[2,2,1024,2048]{3,2,1,0:T(8,128)(2,1)} %bitcast.250, bf16[2,2,1024,2048]{3,2,1,0:T(8,128)(2,1)} %bitcast.251, ...), custom_call_target="tpu_custom_call" | custom-call | flops 34359738368 | bytes 34359736 | tf_op jit(solution)/shard_map/pallas_call | solution.py:92
  1830.0 37.7 %collective-permute-done.89.refs_10_ = bf16[4096,256]{1,0:T(8,128)(2,1)} collective-permute-done((bf16[4096,256]{1,0:T(8,128)(2,1)}, bf16[4096,256]{1,0:T(8,128)(2,1)}, u32[]{:S(2)}, u32[]{:S(2)}) %collective-permute-start.89) | collective-permute-done | bytes 2097184 | tf_op jit(solution)/shard_map/ppermute | solution.py:46
  2023.6 59.4 %collective-permute-done.83 = f32[2048,512]{1,0:T(8,128)} collective-permute-done((f32[2048,512]{1,0:T(8,128)}, f32[2048,512]{1,0:T(8,128)}, u32[]{:S(2)}, u32[]{:S(2)}) %collective-permute-start.83) | collective-permute-done | bytes 4194336 | tf_op jit(solution)/shard_map/ppermute | solution.py:46
  2089.2 83.5 %collective-permute-done.87 = f32[2048,512]{1,0:T(8,128)S(1)} collective-permute-done((f32[2048,512]{1,0:T(8,128)}, f32[2048,512]{1,0:T(8,128)S(1)}, u32[]{:S(2)}, u32[]{:S(2)}) %collective-permute-start.87) | collective-permute-done | bytes 4194336 | tf_op jit(solution)/shard_map/ppermute | solution.py:46
  2175.5 41.3 %collective-permute-done.93 = f32[1024,512]{1,0:T(8,128)S(1)} collective-permute-done((f32[1024,512]{1,0:T(8,128)S(1)}, f32[1024,512]{1,0:T(8,128)S(1)}, u32[]{:S(2)}, u32[]{:S(2)}) %collective-permute-start.93) | collective-permute-done | bytes 2097184 | tf_op jit(solution)/shard_map/ppermute | solution.py:46
  (410 shorter events, 1038.8 us)
Async XLA Ops:
  3.3 161.3 %collective-permute-start = (bf16[1024,2048]{1,0:T(8,128)(2,1)}, bf16[1024,2048]{1,0:T(8,128)(2,1)}, u32[]{:S(2)}, u32[]{:S(2)}) collective-permute-start(bf16[1024,2048]{1,0:T(8,128)(2,1)} %param.11), channel_id=1, source_target_pairs={{0,4},{4,0},{1,5},{5,1},{2,6},{6,2},{3,7},{7,3}} | collective-permute-start | bytes 12582920 | tf_op jit(solution)/shard_map/ppermute | solution.py:46
  11.9 160.7 %collective-permute-start.8 = (bf16[1024,1024]{1,0:T(8,128)(2,1)}, bf16[1024,1024]{1,0:T(8,128)(2,1)}, u32[]{:S(2)}, u32[]{:S(2)}) collective-permute-start(bf16[1024,1024]{1,0:T(8,128)(2,1)} %get-tuple-element.79), channel_id=1, source_target_pairs={{0,2},{2,0},{1,3},{3,1},{4,6},{6,4},{5,7},{7,5}} | collective-permute-start | bytes 6291464 | tf_op jit(solution)/shard_map/ppermute | solution.py:46
  13.6 195.9 %collective-permute-start.4 = (bf16[1024,512]{1,0:T(8,128)(2,1)}, bf16[1024,512]{1,0:T(8,128)(2,1)}, u32[]{:S(2)}, u32[]{:S(2)}) collective-permute-start(bf16[1024,512]{1,0:T(8,128)(2,1)} %pad_maximum_fusion.10.refs_4_), channel_id=1, source_target_pairs={{0,2},{2,0},{1,3},{3,1},{4,6},{6,4},{5,7},{7,5}} | collective-permute-start | bytes 3145736 | tf_op jit(solution)/shard_map/ppermute | solution.py:46
  15.7 146.1 %collective-permute-start.6 = (s32[2,1024]{1,0:T(2,128)}, s32[2,1024]{1,0:T(2,128)}, u32[]{:S(2)}, u32[]{:S(2)}) collective-permute-start(s32[2,1024]{1,0:T(2,128)} %pad_add_fusion), channel_id=1, source_target_pairs={{0,2},{2,0},{1,3},{3,1},{4,6},{6,4},{5,7},{7,5}} | collective-permute-start | bytes 24584 | tf_op jit(solution)/shard_map/ppermute | solution.py:46
  211.0 185.4 %collective-permute-start.10 = (bf16[1024,4096]{1,0:T(8,128)(2,1)}, bf16[1024,4096]{1,0:T(8,128)(2,1)}, u32[]{:S(2)}, u32[]{:S(2)}) collective-permute-start(bf16[1024,4096]{1,0:T(8,128)(2,1)} %get-tuple-element.66), channel_id=1, source_target_pairs={{0,1},{1,0},{2,3},{3,2},{4,5},{5,4},{6,7},{7,6}} | collective-permute-start | bytes 25165832 | tf_op jit(solution)/shard_map/ppermute | solution.py:46
  245.5 150.9 %collective-permute-start.13 = (bf16[1024,4096]{1,0:T(8,128)(2,1)}, bf16[1024,4096]{1,0:T(8,128)(2,1)}, u32[]{:S(2)}, u32[]{:S(2)}) collective-permute-start(bf16[1024,4096]{1,0:T(8,128)(2,1)} %get-tuple-element.64), channel_id=1, source_target_pairs={{0,1},{1,0},{2,3},{3,2},{4,5},{5,4},{6,7},{7,6}} | collective-permute-start | bytes 25165832 | tf_op jit(solution)/shard_map/ppermute | solution.py:46
  394.6 136.7 %collective-permute-start.26 = (bf16[1024,1024]{1,0:T(8,128)(2,1)}, bf16[1024,1024]{1,0:T(8,128)(2,1)}, u32[]{:S(2)}, u32[]{:S(2)}) collective-permute-start(bf16[1024,1024]{1,0:T(8,128)(2,1)} %get-tuple-element.51), channel_id=1, source_target_pairs={{0,2},{2,0},{1,3},{3,1},{4,6},{6,4},{5,7},{7,5}} | collective-permute-start | bytes 6291464 | tf_op jit(solution)/shard_map/ppermute | solution.py:46
  531.3 229.3 %collective-permute-start.29 = (bf16[4096,1024]{1,0:T(8,128)(2,1)}, bf16[4096,1024]{1,0:T(8,128)(2,1)}, u32[]{:S(2)}, u32[]{:S(2)}) collective-permute-start(bf16[4096,1024]{1,0:T(8,128)(2,1)} %get-tuple-element.46), channel_id=1, source_target_pairs={{0,1},{1,0},{2,3},{3,2},{4,5},{5,4},{6,7},{7,6}} | collective-permute-start | bytes 25165832 | tf_op jit(solution)/shard_map/ppermute | solution.py:46
  824.2 150.9 %collective-permute-start.38 = (f32[2048,512]{1,0:T(8,128)}, f32[2048,512]{1,0:T(8,128)}, u32[]{:S(2)}, u32[]{:S(2)}) collective-permute-start(f32[2048,512]{1,0:T(8,128)} %get-tuple-element.24), channel_id=1, source_target_pairs={{0,4},{4,0},{1,5},{5,1},{2,6},{6,2},{3,7},{7,3}} | collective-permute-start | bytes 12582920 | tf_op jit(solution)/shard_map/ppermute | solution.py:46
  891.2 173.8 %collective-permute-start.42 = (f32[2048,512]{1,0:T(8,128)}, f32[2048,512]{1,0:T(8,128)}, u32[]{:S(2)}, u32[]{:S(2)}) collective-permute-start(f32[2048,512]{1,0:T(8,128)} %get-tuple-element.26), channel_id=1, source_target_pairs={{0,4},{4,0},{1,5},{5,1},{2,6},{6,2},{3,7},{7,3}} | collective-permute-start | bytes 12582920 | tf_op jit(solution)/shard_map/ppermute | solution.py:46
  895.9 175.7 %collective-permute-start.46 = (f32[1024,512]{1,0:T(8,128)}, f32[1024,512]{1,0:T(8,128)}, u32[]{:S(2)}, u32[]{:S(2)}) collective-permute-start(f32[1024,512]{1,0:T(8,128)} %slice.232), channel_id=1, source_target_pairs={{0,2},{2,0},{1,3},{3,1},{4,6},{6,4},{5,7},{7,5}} | collective-permute-start | bytes 6291464 | tf_op jit(solution)/shard_map/ppermute | solution.py:46
  909.1 200.1 %collective-permute-start.48 = (f32[1024,512]{1,0:T(8,128)S(1)}, f32[1024,512]{1,0:T(8,128)}, u32[]{:S(2)}, u32[]{:S(2)}) collective-permute-start(f32[1024,512]{1,0:T(8,128)S(1)} %slice_add_fusion.7), channel_id=1, source_target_pairs={{0,4},{4,0},{1,5},{5,1},{2,6},{6,2},{3,7},{7,3}} | collective-permute-start | bytes 6291464 | tf_op jit(solution)/shard_map/ppermute | solution.py:46
  915.7 196.6 %collective-permute-start.35 = (f32[1024,512]{1,0:T(8,128)}, f32[1024,512]{1,0:T(8,128)}, u32[]{:S(2)}, u32[]{:S(2)}) collective-permute-start(f32[1024,512]{1,0:T(8,128)} %slice.282), channel_id=1, source_target_pairs={{0,2},{2,0},{1,3},{3,1},{4,6},{6,4},{5,7},{7,5}} | collective-permute-start | bytes 6291464 | tf_op jit(solution)/shard_map/ppermute | solution.py:46
  1137.3 136.3 %collective-permute-start.50 = (bf16[1024,2048]{1,0:T(8,128)(2,1)S(1)}, bf16[1024,2048]{1,0:T(8,128)(2,1)S(1)}, u32[]{:S(2)}, u32[]{:S(2)}) collective-permute-start(bf16[1024,2048]{1,0:T(8,128)(2,1)S(1)} %multiply_convert_fusion), channel_id=1, source_target_pairs={{0,4},{4,0},{1,5},{5,1},{2,6},{6,2},{3,7},{7,3}} | collective-permute-start | bytes 12582920 | tf_op jit(solution)/shard_map/ppermute | solution.py:46
  1273.6 171.2 %collective-permute-start.59 = (bf16[1024,1024]{1,0:T(8,128)(2,1)}, bf16[1024,1024]{1,0:T(8,128)(2,1)}, u32[]{:S(2)}, u32[]{:S(2)}) collective-permute-start(bf16[1024,1024]{1,0:T(8,128)(2,1)} %get-tuple-element.50), channel_id=1, source_target_pairs={{0,2},{2,0},{1,3},{3,1},{4,6},{6,4},{5,7},{7,5}} | collective-permute-start | bytes 6291464 | tf_op jit(solution)/shard_map/ppermute | solution.py:46
  1317.3 186.4 %collective-permute-start.55 = (bf16[1024,4096]{1,0:T(8,128)(2,1)}, bf16[1024,4096]{1,0:T(8,128)(2,1)}, u32[]{:S(2)}, u32[]{:S(2)}) collective-permute-start(bf16[1024,4096]{1,0:T(8,128)(2,1)} %get-tuple-element.65), channel_id=1, source_target_pairs={{0,1},{1,0},{2,3},{3,2},{4,5},{5,4},{6,7},{7,6}} | collective-permute-start | bytes 25165832 | tf_op jit(solution)/shard_map/ppermute | solution.py:46
  1324.9 178.9 %collective-permute-start.58 = (bf16[1024,4096]{1,0:T(8,128)(2,1)}, bf16[1024,4096]{1,0:T(8,128)(2,1)}, u32[]{:S(2)}, u32[]{:S(2)}) collective-permute-start(bf16[1024,4096]{1,0:T(8,128)(2,1)} %get-tuple-element.63), channel_id=1, source_target_pairs={{0,1},{1,0},{2,3},{3,2},{4,5},{5,4},{6,7},{7,6}} | collective-permute-start | bytes 25165832 | tf_op jit(solution)/shard_map/ppermute | solution.py:46
  1502.4 136.7 %collective-permute-start.71 = (bf16[1024,1024]{1,0:T(8,128)(2,1)}, bf16[1024,1024]{1,0:T(8,128)(2,1)}, u32[]{:S(2)}, u32[]{:S(2)}) collective-permute-start(bf16[1024,1024]{1,0:T(8,128)(2,1)} %get-tuple-element.47), channel_id=1, source_target_pairs={{0,2},{2,0},{1,3},{3,1},{4,6},{6,4},{5,7},{7,5}} | collective-permute-start | bytes 6291464 | tf_op jit(solution)/shard_map/ppermute | solution.py:46
  1639.0 229.2 %collective-permute-start.74 = (bf16[4096,1024]{1,0:T(8,128)(2,1)}, bf16[4096,1024]{1,0:T(8,128)(2,1)}, u32[]{:S(2)}, u32[]{:S(2)}) collective-permute-start(bf16[4096,1024]{1,0:T(8,128)(2,1)} %get-tuple-element.45), channel_id=1, source_target_pairs={{0,1},{1,0},{2,3},{3,2},{4,5},{5,4},{6,7},{7,6}} | collective-permute-start | bytes 25165832 | tf_op jit(solution)/shard_map/ppermute | solution.py:46
  1930.8 152.2 %collective-permute-start.83 = (f32[2048,512]{1,0:T(8,128)}, f32[2048,512]{1,0:T(8,128)}, u32[]{:S(2)}, u32[]{:S(2)}) collective-permute-start(f32[2048,512]{1,0:T(8,128)} %get-tuple-element.32), channel_id=1, source_target_pairs={{0,4},{4,0},{1,5},{5,1},{2,6},{6,2},{3,7},{7,3}} | collective-permute-start | bytes 12582920 | tf_op jit(solution)/shard_map/ppermute | solution.py:46
  2000.1 172.6 %collective-permute-start.87 = (f32[2048,512]{1,0:T(8,128)}, f32[2048,512]{1,0:T(8,128)S(1)}, u32[]{:S(2)}, u32[]{:S(2)}) collective-permute-start(f32[2048,512]{1,0:T(8,128)} %get-tuple-element.34), channel_id=1, source_target_pairs={{0,4},{4,0},{1,5},{5,1},{2,6},{6,2},{3,7},{7,3}} | collective-permute-start | bytes 12582920 | tf_op jit(solution)/shard_map/ppermute | solution.py:46
  2004.1 171.4 %collective-permute-start.91 = (f32[1024,512]{1,0:T(8,128)}, f32[1024,512]{1,0:T(8,128)}, u32[]{:S(2)}, u32[]{:S(2)}) collective-permute-start(f32[1024,512]{1,0:T(8,128)} %slice.261), channel_id=1, source_target_pairs={{0,2},{2,0},{1,3},{3,1},{4,6},{6,4},{5,7},{7,5}} | collective-permute-start | bytes 6291464 | tf_op jit(solution)/shard_map/ppermute | solution.py:46
  2016.7 200.0 %collective-permute-start.93 = (f32[1024,512]{1,0:T(8,128)S(1)}, f32[1024,512]{1,0:T(8,128)S(1)}, u32[]{:S(2)}, u32[]{:S(2)}) collective-permute-start(f32[1024,512]{1,0:T(8,128)S(1)} %slice_add_fusion.6), channel_id=1, source_target_pairs={{0,4},{4,0},{1,5},{5,1},{2,6},{6,2},{3,7},{7,3}} | collective-permute-start | bytes 6291464 | tf_op jit(solution)/shard_map/ppermute | solution.py:46
  2022.2 197.1 %collective-permute-start.80 = (f32[1024,512]{1,0:T(8,128)}, f32[1024,512]{1,0:T(8,128)S(1)}, u32[]{:S(2)}, u32[]{:S(2)}) collective-permute-start(f32[1024,512]{1,0:T(8,128)} %slice.306), channel_id=1, source_target_pairs={{0,2},{2,0},{1,3},{3,1},{4,6},{6,4},{5,7},{7,5}} | collective-permute-start | bytes 6291464 | tf_op jit(solution)/shard_map/ppermute | solution.py:46
  (136 other events, 7330.7 us)

commit v2 on v1

--- a/solution.py
+++ b/solution.py
@@ -50,16 +50,16 @@
     return jnp.dot(a, b, preferred_element_type=jnp.float32)
 
 
-def in_kernel(gated, idx_ref, *refs):
-    h_refs, refs, out_ref = refs[0:4], refs[4:-1], refs[-1]
-    rows = h_refs[0].shape[1]
-    for block in range(2):
+def in_kernel(gated, blocks, idx_ref, *refs):
+    h_all, refs, out_ref = refs[0:4 * blocks], refs[4 * blocks:-1], refs[-1]
+    rows = h_all[0].shape[0]
+    for block in range(blocks):
         sl = slice(block * rows, (block + 1) * rows)
 
         def product(pieces):
             total = None
-            for h_ref, piece in zip(h_refs, pieces):
-                term = dot32(h_ref[block], piece[...])
+            for h_ref, piece in zip(h_all[4 * block:4 * block + 4], pieces):
+                term = dot32(h_ref[...], piece[...])
                 total = term if total is None else total + term
             return total.astype(jnp.bfloat16)
 
@@ -72,16 +72,16 @@
 
 
 def in_proj(idx, h, pieces, maps, n_cols, gated, tile=256):
-    _, blocks, block_tok, half = h.shape
-    tokens, width, depth = blocks * block_tok, 2 * half, half // 2
+    _, block_tok, half = h[0].shape
+    tokens, width, depth = len(h) * block_tok, 2 * half, half // 2
     once = dict(pipeline_mode=pl.Buffered(1))
-    h_block = (None, blocks, block_tok, depth)
+    h_block = (None, block_tok, depth)
     specs = [
-        pl.BlockSpec(h_block, lambda i, s: (1 - s[1], 0, 0, s[2]), **once),
-        pl.BlockSpec(h_block, lambda i, s: (1 - s[1], 0, 0, 1 - s[2]), **once),
-        pl.BlockSpec(h_block, lambda i, s: (s[1], 0, 0, s[2]), **once),
-        pl.BlockSpec(h_block, lambda i, s: (s[1], 0, 0, 1 - s[2]), **once),
-    ]
+        pl.BlockSpec(h_block, lambda i, s: (1 - s[1], 0, s[2]), **once),
+        pl.BlockSpec(h_block, lambda i, s: (1 - s[1], 0, 1 - s[2]), **once),
+        pl.BlockSpec(h_block, lambda i, s: (s[1], 0, s[2]), **once),
+        pl.BlockSpec(h_block, lambda i, s: (s[1], 0, 1 - s[2]), **once),
+    ] * len(h)
     for piece, fn in zip(pieces, maps):
         if piece.ndim == 3:
             layer, col = fn
@@ -90,7 +90,7 @@
             specs.append(pl.BlockSpec((depth, tile), functools.partial(lambda i, s, col: (0, col(i, s)), col=fn)))
     flops = 2 * tokens * width * n_cols * (2 if gated else 1)
     return pl.pallas_call(
-        functools.partial(in_kernel, gated),
+        functools.partial(in_kernel, gated, len(h)),
         grid_spec=pltpu.PrefetchScalarGridSpec(
             num_scalar_prefetch=1,
             grid=(n_cols // tile,),
@@ -100,7 +100,7 @@
         out_shape=jax.ShapeDtypeStruct((tokens, n_cols), jnp.bfloat16),
         compiler_params=pltpu.CompilerParams(vmem_limit_bytes=VMEM_LIMIT),
         cost_estimate=pl.CostEstimate(flops=flops, bytes_accessed=flops // 1000, transcendentals=0),
-    )(idx, h, h, h, h, *pieces)
+    )(idx, *[v for v in h for _ in range(4)], *pieces)
 
 
 def back_kernel(idx_ref, *refs):
@@ -159,6 +159,65 @@
     )(idx, *acts, w_out, w_down, *own_p, *recv, *recv_p)
 
 
+def split_back_kernel(idx_ref, *refs):
+    out_ref, weights = refs[-1], refs[-17:-1]
+    num = (len(refs) - 17) // 2
+    acts = refs[:2 * num]
+    width = weights[0].shape[-1]
+
+    def product(piece):
+        total = None
+        for q in range(2):
+            wo, wd = weights[8 * q + 2 * piece], weights[8 * q + 2 * piece + 1]
+            total_q = dot32(acts[num * q][...], wo[...])
+            total = total_q if total is None else total + total_q
+            off = 0
+            for act in acts[num * q + 1:num * (q + 1)]:
+                total = total + dot32(act[...], wd[off:off + act.shape[1], :])
+                off += act.shape[1]
+        return total
+
+    same = idx_ref[1] == 1
+    outs = [product(p) for p in range(4)]
+    for flag, order in ((same, (2, 3, 0, 1)), (jnp.logical_not(same), (0, 1, 2, 3))):
+        @pl.when(flag)
+        def _():
+            for p in range(4):
+                out_ref[:, p * width:(p + 1) * width] = outs[order[p]]
+
+
+def split_back_proj(idx, acts, acts_y, w_out, w_down, mine, foreign, layer, w, rows=256):
+    blocks, _, half_tok, depth = acts[0].shape
+    width = mine[3].shape[1]
+    tiles = half_tok // rows
+    once = dict(pipeline_mode=pl.Buffered(1))
+    specs = [pl.BlockSpec((None, None, rows, act.shape[-1]), lambda i, s: (i // tiles, s[3], i % tiles, 0)) for act in acts]
+    specs += [pl.BlockSpec((None, rows, act.shape[-1]), lambda i, s: (i // tiles, i % tiles, 0)) for act in acts_y]
+    specs.append(pl.BlockSpec((None, depth, width), lambda i, s: (layer, s[0], w), **once))
+    specs.append(pl.BlockSpec((None, 4 * depth, width), lambda i, s: (layer, s[0], w), **once))
+    for arr in (*mine, *foreign):
+        whole = arr.shape[1] > width
+        specs.append(pl.BlockSpec((arr.shape[0], width), (lambda i, s: (0, w)) if whole else (lambda i, s: (0, 0)), **once))
+    flops = 2 * blocks * half_tok * 10 * depth * 4 * width
+    return pl.pallas_call(
+        split_back_kernel,
+        grid_spec=pltpu.PrefetchScalarGridSpec(
+            num_scalar_prefetch=1,
+            grid=(blocks * tiles,),
+            in_specs=specs,
+            out_specs=pl.BlockSpec((None, rows, 4 * width), lambda i, s: (i // tiles, i % tiles, 0)),
+        ),
+        out_shape=jax.ShapeDtypeStruct((blocks, half_tok, 4 * width), jnp.float32),
+        compiler_params=pltpu.CompilerParams(vmem_limit_bytes=VMEM_LIMIT),
+        cost_estimate=pl.CostEstimate(flops=flops, bytes_accessed=flops // 1000, transcendentals=0),
+    )(idx, *acts, *acts_y, w_out, w_down, *mine, *foreign)
+
+
+def gu_widths(layer, hidden):
+    unit = hidden // CHUNKS
+    return [unit] * CHUNKS if layer == 0 else [unit] * (CHUNKS - 1) + [unit // 2] * 2
+
+
 def solution(mesh):
     def device_body(x_loc, seg_ids, pos_ids, w_q, w_k, w_v, w_gate, w_up, w_out, w_down, gain):
         tb = lax.axis_index("tb")
@@ -170,9 +229,8 @@
         head_dim = w_k.shape[-1]
         nq = w_q.shape[-1] // 2
         nf = w_gate.shape[-1] // 2
-        cin = nf // CHUNKS
         cbk = w_out.shape[-1] // CHUNKS
-        idx = jnp.stack([tb, (tb == mp).astype(jnp.int32), ta]).astype(jnp.int32)
+        idx = jnp.stack([tb, (tb == mp).astype(jnp.int32), ta, mp]).astype(jnp.int32)
 
         def part(w, l, r0, nr, c0, nc):
             return lax.dynamic_slice(w, (l, r0, c0), (1, nr, nc))[0]
@@ -189,26 +247,32 @@
         ids = jnp.stack([seg_ids, pos_ids])
         ids_f = hop(ids, "tb")
         segs, poss = (ids[0], ids_f[0]), (ids[1], ids_f[1])
-        cos_tab, sin_tab = rope_tables(jnp.concatenate(poss), head_dim)
+        tables = [rope_tables(p, head_dim) for p in poss]
         hidden = x_loc.astype(jnp.float32)
         kv_own = jnp.concatenate([w for l in range(layers) for w in (w_k[l], w_v[l])], axis=1)
-        kv_recv = hop(kv_own, "tb")
+        kv_x = hop(lax.dynamic_slice_in_dim(kv_own, mp * 2 * head_dim, 2 * head_dim, axis=1), "tb")
+        kv_y = hop(kv_x, "mp")
+        kv_recv = jnp.where(mp == 0, jnp.concatenate([kv_x, kv_y], axis=1), jnp.concatenate([kv_y, kv_x], axis=1))
         kv_p = hop(kv_own, "ta")
         kv_e = hop(kv_recv, "ta")
         for l in range(layers):
             q_p = hop(part(w_q, l, 0, quarter, tb * nq, nq), "ta")
             g_p = hop(part(w_gate, l, 0, quarter, tb * nf, nf), "ta")
             u_p = hop(part(w_up, l, 0, quarter, tb * nf, nf), "ta")
-            o_p = hop(part(w_out, l, tb * nq, nq, 0, quarter), "ta")
-            d_p = hop(part(w_down, l, tb * nf, nf, 0, quarter), "ta")
+            o_own = part(w_out, l, tb * nq, nq, 0, quarter)
+            d_own = part(w_down, l, tb * nf, nf, 0, quarter)
+            o_p = hop(o_own, "ta")
+            d_p = hop(d_own, "ta")
             q_x = hop(part(w_q, l, 0, quarter, (1 - tb) * nq, nq), "tb")
-            g_x = [hop(part(w_gate, l, 0, quarter, (1 - tb) * nf + j * cin, cin), "tb") for j in range(CHUNKS)]
-            u_x = [hop(part(w_up, l, 0, quarter, (1 - tb) * nf + j * cin, cin), "tb") for j in range(CHUNKS)]
+            widths = gu_widths(l, nf)
+            offs = [sum(widths[:j]) for j in range(len(widths))]
+            g_x = [hop(part(w_gate, l, 0, quarter, (1 - tb) * nf + off, n), "tb") for off, n in zip(offs, widths)]
+            u_x = [hop(part(w_up, l, 0, quarter, (1 - tb) * nf + off, n), "tb") for off, n in zip(offs, widths)]
             o_x = hop(part(w_out, l, (1 - tb) * nq, nq, 0, quarter), "tb")
             d_x = [hop(part(w_down, l, (1 - tb) * nf, nf, w * cbk, cbk), "tb") for w in range(CHUNKS)]
             q_e = hop(q_x, "ta")
-            g_e = [hop(g_x[j], "ta") for j in range(CHUNKS)]
-            u_e = [hop(u_x[j], "ta") for j in range(CHUNKS)]
+            g_e = [hop(v, "ta") for v in g_x]
+            u_e = [hop(v, "ta") for v in u_x]
             o_e = hop(o_x, "ta")
             d_e = [hop(d_x[w], "ta") for w in range(CHUNKS)]
 
@@ -220,43 +284,61 @@
             else:
                 mean_sq = lax.psum(jnp.sum(hidden * hidden, axis=-1, keepdims=True), "mp") / (2 * half)
                 sides = gather_rows((hidden * lax.rsqrt(mean_sq + NORM_EPS) * gain_half(l, mp)).astype(jnp.bfloat16))
-            h = jnp.concatenate([v for side in sides for v in side], axis=0).reshape(2, 2, num_tok, half)
+            h = []
+            for t in range(2):
+                h.append(jnp.concatenate([sides[0][t], sides[1][t]], axis=0).reshape(2, num_tok, half))
 
             tile = 256
-            qt, ct, ft = nq // tile, cin // tile, nf // tile
+            qt, ft = nq // tile, nf // tile
             step = lambda i, s: i
-            q = in_proj(idx, h, [w_q, q_p, q_x, q_e], [(l, lambda i, s: s[0] * qt + i), step, step, step], nq, False)
-            kv = in_proj(idx, h, [kv_own, kv_p, kv_recv, kv_e], [lambda i, s, l=l: l] * 4, tile, False)
-            q_rot = apply_rope(q.reshape(2 * num_tok, nq // head_dim, head_dim), cos_tab[:, None, :], sin_tab[:, None, :])
-            k_rot = apply_rope(kv[:, :head_dim], cos_tab, sin_tab)
-            v_proj = kv[:, head_dim:]
             blocks = []
             for t in range(2):
-                sl = slice(t * num_tok, (t + 1) * num_tok)
-                blocks.append(block_attention(q_rot[sl], k_rot[sl], v_proj[sl], segs[t], poss[t]).reshape(num_tok, nq))
+                q = in_proj(idx, h[t:t + 1], [w_q, q_p, q_x, q_e], [(l, lambda i, s: s[0] * qt + i), step, step, step], nq, False)
+                kv = in_proj(idx, h[t:t + 1], [kv_own, kv_p, kv_recv, kv_e], [lambda i, s, l=l: l] * 4, tile, False)
+                if t == 1:
+                    kv, k_rot = lax.optimization_barrier((kv, k_rot))
+                cos_tab, sin_tab = tables[t]
+                q_rot = apply_rope(q.reshape(num_tok, nq // head_dim, head_dim), cos_tab[:, None, :], sin_tab[:, None, :])
+                k_rot = apply_rope(kv[:, :head_dim], cos_tab, sin_tab)
+                blocks.append(block_attention(q_rot, k_rot, kv[:, head_dim:], segs[t], poss[t]).reshape(num_tok, nq))
             acts = [jnp.concatenate(blocks, axis=0)]
-            for j in range(CHUNKS):
-                own_map = (l, functools.partial(lambda i, s, j: s[0] * ft + j * ct + i, j=j))
-                p_map = functools.partial(lambda i, s, j: j * ct + i, j=j)
+            for j, (off, n) in enumerate(zip(offs, widths)):
+                own_map = (l, functools.partial(lambda i, s, o: s[0] * ft + o + i, o=off // tile))
+                p_map = functools.partial(lambda i, s, o: o + i, o=off // tile)
                 acts.append(in_proj(
                     idx, h, [w_gate, g_p, g_x[j], g_e[j], w_up, u_p, u_x[j], u_e[j]],
-                    [own_map, p_map, step, step] * 2, cin, True))
-            parts_a, parts_b = [], []
-            for w in range(CHUNKS):
+                    [own_map, p_map, step, step] * 2, n, True))
+
+            def place(res, d, w):
+                for k, core in enumerate((ta, 1 - ta)):
+                    col = core * quarter + w * cbk
+                    part_k = lax.dynamic_slice_in_dim(res, col, cbk, axis=1) + d[:, k * cbk:(k + 1) * cbk]
+                    res = lax.dynamic_update_slice_in_dim(res, part_k, col, axis=1)
+                return res
+
+            if l == layers - 1:
+                half_tok = num_tok // 2
+                o_y, d_y = hop(o_own, "mp"), hop(d_own, "mp")
+                o_yp, d_yp = hop(o_y, "ta"), hop(d_y, "ta")
+                o_xy = hop(o_x, "mp")
+                o_xye = hop(o_xy, "ta")
+                acts = [act.reshape(2, 2, half_tok, -1) for act in acts]
+                acts_y = [hop(lax.dynamic_index_in_dim(act, 1 - mp, axis=1, keepdims=False), "mp") for act in acts]
+                for w in range(CHUNKS):
+                    d_xy = hop(d_x[w], "mp")
+                    d_xye = hop(d_xy, "ta")
+                    out = split_back_proj(idx, acts, acts_y, w_out, w_down, [o_p, d_p, o_x, d_x[w], o_e, d_e[w]], [o_y, d_y, o_yp, d_yp, o_xy, d_xy, o_xye, d_xye], l, w)
+                    total = out[0] + hop(out[1], "tb")
+                    kept = total[:, 2 * cbk:]
+                    came = hop(total[:, :2 * cbk], "mp")
+                    low = mp == 0
+                    d = jnp.concatenate([jnp.where(low, kept, came), jnp.where(low, came, kept)], axis=0)
+                    hidden = place(hidden, d, w)
+            for w in range(CHUNKS if l < layers - 1 else 0):
                 send, keep = back_proj(idx, acts, w_out, w_down, (o_p, d_p), (o_x, d_x[w]), (o_e, d_e[w]), l, w)
-                if w < CHUNKS - 1:
-                    summed = keep + hop(send, "mp")
-                    d = summed[:num_tok] + hop(summed[num_tok:], "tb")
-                else:
-                    passed = send[:num_tok] + hop(send[num_tok:], "tb")
-                    kept = keep[:num_tok] + hop(keep[num_tok:], "tb")
-                    d = kept + hop(passed, "mp")
-                parts_a.append(d[:, :cbk])
-                parts_b.append(d[:, cbk:])
-            first = ta == 0
-            pa = jnp.concatenate(parts_a, axis=1)
-            pb = jnp.concatenate(parts_b, axis=1)
-            hidden = hidden + jnp.concatenate([jnp.where(first, pa, pb), jnp.where(first, pb, pa)], axis=1)
+                summed = keep + hop(send, "mp")
+                d = summed[:num_tok] + hop(summed[num_tok:], "tb")
+                hidden = place(hidden, d, w)
         return hidden
 
     col_spec = P(None, PLANE_AXES, "mp")

time: 2250 us -> 2740 us (1.22)
  waiting for transfers between devices: 1050 us -> 1480 us
  Pallas kernels: 686 us -> 723 us
    ppermute x94 -> x117, waiting for transfers between devices: 1050 us -> 1480 us  [hop(): return lax.ppermute(val, axis, SWAP)]
    pallas_call x12 -> x21, Pallas kernels: 439 us -> 599 us  [the longest x17 464 us: in_proj(): pl.pallas_call(functools.partial(in_kernel, gated, len(h)), grid_spec=plt...]
    pallas_call x8 -> x4, Pallas kernels: 247 us -> 124 us  [back_proj(): pl.pallas_call(back_kernel, grid_spec=pltpu.PrefetchScalarGridSpec(num_sc...]
    ppermute x94 -> x117, starting transfers between devices: 75.5 us -> 86.5 us  [hop(): return lax.ppermute(val, axis, SWAP)]
    squeeze x8 -> x10, local copies, waits for them, and re-layouts: 80.9 us -> 84.2 us  [part(): return lax.dynamic_slice(w, (l, r0, c0), (1, nr, nc))[0]]
  transfers between devices with their start and end apart: 94 -> 117, of which waited for: 28 -> 39; matrix products, arithmetic and copies ran while one was open for 17% -> 15% of each run, Pallas kernels for 31% -> 26%
where the time goes in v2:
time: 2740 us; the launch traced here: 2730 us
  waiting for transfers between devices  1480 us (54%)
  Pallas kernels  723 us (26%)
  local copies, waits for them, and re-layouts  164 us (6%)
  other arithmetic  137 us (5%)
  matrix products  134 us (5%)
  starting transfers between devices  86.5 us (3%)
    ppermute x117, waiting for transfers between devices, hop(): return lax.ppermute(val, axis, SWAP)  1480 us
    pallas_call x17, Pallas kernels, in_proj(): pl.pallas_call(functools.partial(in_kernel, gated, len(h)), grid_spec=plt...  464 us
    pallas_call x4, Pallas kernels, split_back_proj(): pl.pallas_call(split_back_kernel, grid_spec=pltpu.PrefetchScalarGridSpec(...  135 us
    pallas_call x4, Pallas kernels, back_proj(): pl.pallas_call(back_kernel, grid_spec=pltpu.PrefetchScalarGridSpec(num_sc...  124 us
    ppermute x117, starting transfers between devices, hop(): return lax.ppermute(val, axis, SWAP)  86.5 us
    squeeze x10, local copies, waits for them, and re-layouts, part(): return lax.dynamic_slice(w, (l, r0, c0), (1, nr, nc))[0]  84.2 us
    sub x4, matrix products, block_attention(): exp_scores = jnp.exp(scores - row_peak)  81.9 us
  transfers between devices with their start and end apart: 117, of which 39 were waited for; matrix products, arithmetic and copies ran while one was open for 15% of the time, Pallas kernels for 26%

profile of v2, /device:TPU:0, one launch (start us, length us, event | category | flops | bytes accessed | tf_op | source)
XLA Modules:
  0.0 2733.9 jit_solution(1210899967168281171)
XLA Ops:
  154.3 43.1 %collective-permute-done.3 = bf16[1024,256]{1,0:T(8,128)(2,1)S(1)} collective-permute-done((bf16[1024,256]{1,0:T(8,128)(2,1)S(1)}, bf16[1024,256]{1,0:T(8,128)(2,1)S(1)}, u32[]{:S(2)}, u32[]{:S(2)}) %collective-permute-start.3) | collective-permute-done | bytes 524320 | tf_op jit(solution)/shard_map/ppermute | solution.py:46
  430.0 45.4 %shard_map.113.refs_1_ = bf16[2048,1024]{1,0:T(8,128)(2,1)} custom-call(s32[4]{0:T(128)} %pad_add_fusion.1.idx_ref, bf16[2,1024,2048]{2,1,0:T(8,128)(2,1)} %bitcast.332, bf16[2,1024,2048]{2,1,0:T(8,128)(2,1)} %bitcast.330, bf16[2,1024,2048]{2,1,0:T(8,128)(2,1)} %bitcast.331, bf16[2,1024,2048]{2,1,0:T(8,128)(2,1)} %bitcast.329, ...), custom_call_target="tpu_custom_call" | custom-call | flops 34359738368 | bytes 34359736 | tf_op jit(solution)/shard_map/pallas_call | solution.py:92
  477.0 43.7 %collective-permute-done.25.refs_10_ = bf16[1024,1024]{1,0:T(8,128)(2,1)} collective-permute-done((bf16[1024,1024]{1,0:T(8,128)(2,1)}, bf16[1024,1024]{1,0:T(8,128)(2,1)}, u32[]{:S(2)}, u32[]{:S(2)}) %collective-permute-start.25) | collective-permute-done | bytes 2097184 | tf_op jit(solution)/shard_map/ppermute | solution.py:46
  521.2 44.4 %collective-permute-done.27.refs_14_ = bf16[1024,1024]{1,0:T(8,128)(2,1)} collective-permute-done((bf16[1024,1024]{1,0:T(8,128)(2,1)}, bf16[1024,1024]{1,0:T(8,128)(2,1)}, u32[]{:S(2)}, u32[]{:S(2)}) %collective-permute-start.27) | collective-permute-done | bytes 2097184 | tf_op jit(solution)/shard_map/ppermute | solution.py:46
  566.1 45.1 %shard_map.114.refs_2_ = bf16[2048,1024]{1,0:T(8,128)(2,1)} custom-call(s32[4]{0:T(128)} %pad_add_fusion.1.idx_ref, bf16[2,1024,2048]{2,1,0:T(8,128)(2,1)} %bitcast.333, bf16[2,1024,2048]{2,1,0:T(8,128)(2,1)} %bitcast.334, bf16[2,1024,2048]{2,1,0:T(8,128)(2,1)} %bitcast.335, bf16[2,1024,2048]{2,1,0:T(8,128)(2,1)} %bitcast.336, ...), custom_call_target="tpu_custom_call" | custom-call | flops 34359738368 | bytes 34359736 | tf_op jit(solution)/shard_map/pallas_call | solution.py:92
  611.8 42.1 %collective-permute-done.45.refs_10_ = bf16[4096,256]{1,0:T(8,128)(2,1)} collective-permute-done((bf16[4096,256]{1,0:T(8,128)(2,1)}, bf16[4096,256]{1,0:T(8,128)(2,1)}, u32[]{:S(2)}, u32[]{:S(2)}) %collective-permute-start.45) | collective-permute-done | bytes 2097184 | tf_op jit(solution)/shard_map/ppermute | solution.py:46
  654.9 45.3 %shard_map.115.refs_3_ = bf16[2048,1024]{1,0:T(8,128)(2,1)} custom-call(s32[4]{0:T(128)} %pad_add_fusion.1.idx_ref, bf16[2,1024,2048]{2,1,0:T(8,128)(2,1)} %bitcast.337, bf16[2,1024,2048]{2,1,0:T(8,128)(2,1)} %bitcast.338, bf16[2,1024,2048]{2,1,0:T(8,128)(2,1)} %bitcast.339, bf16[2,1024,2048]{2,1,0:T(8,128)(2,1)} %bitcast.340, ...), custom_call_target="tpu_custom_call" | custom-call | flops 34359738368 | bytes 34359736 | tf_op jit(solution)/shard_map/pallas_call | solution.py:92
  702.8 45.1 %shard_map.116.refs_4_ = bf16[2048,1024]{1,0:T(8,128)(2,1)} custom-call(s32[4]{0:T(128)} %pad_add_fusion.1.idx_ref, bf16[2,1024,2048]{2,1,0:T(8,128)(2,1)} %bitcast.341, bf16[2,1024,2048]{2,1,0:T(8,128)(2,1)} %bitcast.342, bf16[2,1024,2048]{2,1,0:T(8,128)(2,1)} %bitcast.343, bf16[2,1024,2048]{2,1,0:T(8,128)(2,1)} %bitcast.344, ...), custom_call_target="tpu_custom_call" | custom-call | flops 34359738368 | bytes 34359736 | tf_op jit(solution)/shard_map/pallas_call | solution.py:92
  747.9 45.2 %collective-permute-done.32.refs_10_ = bf16[4096,256]{1,0:T(8,128)(2,1)} collective-permute-done((bf16[4096,256]{1,0:T(8,128)(2,1)}, bf16[4096,256]{1,0:T(8,128)(2,1)}, u32[]{:S(2)}, u32[]{:S(2)}) %collective-permute-start.32) | collective-permute-done | bytes 2097184 | tf_op jit(solution)/shard_map/ppermute | solution.py:46
  927.6 85.4 %collective-permute-done.35 = f32[2048,512]{1,0:T(8,128)} collective-permute-done((f32[2048,512]{1,0:T(8,128)}, f32[2048,512]{1,0:T(8,128)}, u32[]{:S(2)}, u32[]{:S(2)}) %collective-permute-start.35) | collective-permute-done | bytes 4194336 | tf_op jit(solution)/shard_map/ppermute | solution.py:46
  1020.6 82.2 %collective-permute-done.39 = f32[2048,512]{1,0:T(8,128)} collective-permute-done((f32[2048,512]{1,0:T(8,128)}, f32[2048,512]{1,0:T(8,128)}, u32[]{:S(2)}, u32[]{:S(2)}) %collective-permute-start.39) | collective-permute-done | bytes 4194336 | tf_op jit(solution)/shard_map/ppermute | solution.py:46
  1123.4 68.8 %collective-permute-done.47 = f32[2048,512]{1,0:T(8,128)} collective-permute-done((f32[2048,512]{1,0:T(8,128)}, f32[2048,512]{1,0:T(8,128)}, u32[]{:S(2)}, u32[]{:S(2)}) %collective-permute-start.47) | collective-permute-done | bytes 4194336 | tf_op jit(solution)/shard_map/ppermute | solution.py:46
  1268.2 44.0 %collective-permute-done.51.refs_6_ = bf16[1024,1024]{1,0:T(8,128)(2,1)S(1)} collective-permute-done((bf16[1024,1024]{1,0:T(8,128)(2,1)}, bf16[1024,1024]{1,0:T(8,128)(2,1)S(1)}, u32[]{:S(2)}, u32[]{:S(2)}) %collective-permute-start.51) | collective-permute-done | bytes 2097184 | tf_op jit(solution)/shard_map/ppermute | solution.py:46
  1361.7 85.4 %collective-permute-done.75.refs_14_ = bf16[1024,512]{1,0:T(8,128)(2,1)} collective-permute-done((bf16[1024,512]{1,0:T(8,128)(2,1)}, bf16[1024,512]{1,0:T(8,128)(2,1)}, u32[]{:S(2)}, u32[]{:S(2)}) %collective-permute-start.75) | collective-permute-done | bytes 1048608 | tf_op jit(solution)/shard_map/ppermute | solution.py:46
  1548.7 43.6 %collective-permute-done.67.refs_14_ = bf16[1024,1024]{1,0:T(8,128)(2,1)} collective-permute-done((bf16[1024,1024]{1,0:T(8,128)(2,1)}, bf16[1024,1024]{1,0:T(8,128)(2,1)}, u32[]{:S(2)}, u32[]{:S(2)}) %collective-permute-start.67) | collective-permute-done | bytes 2097184 | tf_op jit(solution)/shard_map/ppermute | solution.py:46
  1593.7 43.4 %collective-permute-done.61.refs_10_ = bf16[1024,1024]{1,0:T(8,128)(2,1)S(1)} collective-permute-done((bf16[1024,1024]{1,0:T(8,128)(2,1)}, bf16[1024,1024]{1,0:T(8,128)(2,1)S(1)}, u32[]{:S(2)}, u32[]{:S(2)}) %collective-permute-start.61) | collective-permute-done | bytes 2097184 | tf_op jit(solution)/shard_map/ppermute | solution.py:46
  1682.2 44.9 %collective-permute-done.56.refs_10_ = bf16[1024,1024]{1,0:T(8,128)(2,1)} collective-permute-done((bf16[1024,1024]{1,0:T(8,128)(2,1)}, bf16[1024,1024]{1,0:T(8,128)(2,1)}, u32[]{:S(2)}, u32[]{:S(2)}) %collective-permute-start.56) | collective-permute-done | bytes 2097184 | tf_op jit(solution)/shard_map/ppermute | solution.py:46
  1727.1 44.9 %collective-permute-done.59.refs_14_ = bf16[1024,1024]{1,0:T(8,128)(2,1)} collective-permute-done((bf16[1024,1024]{1,0:T(8,128)(2,1)}, bf16[1024,1024]{1,0:T(8,128)(2,1)}, u32[]{:S(2)}, u32[]{:S(2)}) %collective-permute-start.59) | collective-permute-done | bytes 2097184 | tf_op jit(solution)/shard_map/ppermute | solution.py:46
  1906.9 44.5 %collective-permute-done.99.refs_17_ = bf16[4096,256]{1,0:T(8,128)(2,1)} collective-permute-done((bf16[4096,256]{1,0:T(8,128)(2,1)}, bf16[4096,256]{1,0:T(8,128)(2,1)}, u32[]{:S(2)}, u32[]{:S(2)}) %collective-permute-start.99) | collective-permute-done | bytes 2097184 | tf_op jit(solution)/shard_map/ppermute | solution.py:46
  1970.8 45.1 %shard_map.127 = bf16[2048,1024]{1,0:T(8,128)(2,1)} custom-call(s32[4]{0:T(128)} %pad_add_fusion.1.idx_ref, bf16[2,1024,2048]{2,1,0:T(8,128)(2,1)} %bitcast.273, bf16[2,1024,2048]{2,1,0:T(8,128)(2,1)} %bitcast.274, bf16[2,1024,2048]{2,1,0:T(8,128)(2,1)} %bitcast.275, bf16[2,1024,2048]{2,1,0:T(8,128)(2,1)} %bitcast.276, bf16[2,1024,2048]{2,1,0:T(8,128)(2,1)} %bitcast.301, ...), custom_call_target="tpu_custom_call" | custom-call | flops 34359738368 | bytes 34359736 | tf_op jit(solution)/shard_map/pallas_call | solution.py:92
  2058.5 45.3 %shard_map.126 = bf16[2048,1024]{1,0:T(8,128)(2,1)} custom-call(s32[4]{0:T(128)} %pad_add_fusion.1.idx_ref, bf16[2,1024,2048]{2,1,0:T(8,128)(2,1)} %bitcast.278, bf16[2,1024,2048]{2,1,0:T(8,128)(2,1)} %bitcast.277, bf16[2,1024,2048]{2,1,0:T(8,128)(2,1)} %bitcast.279, bf16[2,1024,2048]{2,1,0:T(8,128)(2,1)} %bitcast.280, bf16[2,1024,2048]{2,1,0:T(8,128)(2,1)} %bitcast.306, ...), custom_call_target="tpu_custom_call" | custom-call | flops 34359738368 | bytes 34359736 | tf_op jit(solution)/shard_map/pallas_call | solution.py:92
  2105.0 45.0 %shard_map.125 = bf16[2048,1024]{1,0:T(8,128)(2,1)} custom-call(s32[4]{0:T(128)} %pad_add_fusion.1.idx_ref, bf16[2,1024,2048]{2,1,0:T(8,128)(2,1)} %bitcast.281, bf16[2,1024,2048]{2,1,0:T(8,128)(2,1)} %bitcast.282, bf16[2,1024,2048]{2,1,0:T(8,128)(2,1)} %bitcast.283, bf16[2,1024,2048]{2,1,0:T(8,128)(2,1)} %bitcast.284, bf16[2,1024,2048]{2,1,0:T(8,128)(2,1)} %bitcast.309, ...), custom_call_target="tpu_custom_call" | custom-call | flops 34359738368 | bytes 34359736 | tf_op jit(solution)/shard_map/pallas_call | solution.py:92
  2233.0 192.0 %collective-permute-done.81.refs_10_ = bf16[2,512,512]{2,1,0:T(8,128)(2,1)S(1)} collective-permute-done((bf16[2,512,512]{2,1,0:T(8,128)(2,1)S(1)}, bf16[2,512,512]{2,1,0:T(8,128)(2,1)S(1)}, u32[]{:S(2)}, u32[]{:S(2)}) %collective-permute-start.81) | collective-permute-done | bytes 1048608 | tf_op jit(solution)/shard_map/ppermute | solution.py:46
  2474.3 42.0 %collective-permute-done.94.refs_25_ = bf16[4096,256]{1,0:T(8,128)(2,1)} collective-permute-done((bf16[4096,256]{1,0:T(8,128)(2,1)}, bf16[4096,256]{1,0:T(8,128)(2,1)}, u32[]{:S(2)}, u32[]{:S(2)}) %collective-permute-start.94) | collective-permute-done | bytes 2097184 | tf_op jit(solution)/shard_map/ppermute | solution.py:46
  (511 shorter events, 1376.5 us)
Async XLA Ops:
  3.3 195.8 %collective-permute-start = (bf16[1024,2048]{1,0:T(8,128)(2,1)}, bf16[1024,2048]{1,0:T(8,128)(2,1)}, u32[]{:S(2)}, u32[]{:S(2)}) collective-permute-start(bf16[1024,2048]{1,0:T(8,128)(2,1)} %param.11), channel_id=1, source_target_pairs={{0,4},{4,0},{1,5},{5,1},{2,6},{6,2},{3,7},{7,3}} | collective-permute-start | bytes 12582920 | tf_op jit(solution)/shard_map/ppermute | solution.py:46
  11.9 194.1 %collective-permute-start.6 = (bf16[1024,1024]{1,0:T(8,128)(2,1)}, bf16[1024,1024]{1,0:T(8,128)(2,1)}, u32[]{:S(2)}, u32[]{:S(2)}) collective-permute-start(bf16[1024,1024]{1,0:T(8,128)(2,1)} %get-tuple-element.63), channel_id=1, source_target_pairs={{0,2},{2,0},{1,3},{3,1},{4,6},{6,4},{5,7},{7,5}} | collective-permute-start | bytes 6291464 | tf_op jit(solution)/shard_map/ppermute | solution.py:46
  231.6 197.9 %collective-permute-start.11 = (bf16[1024,4096]{1,0:T(8,128)(2,1)}, bf16[1024,4096]{1,0:T(8,128)(2,1)}, u32[]{:S(2)}, u32[]{:S(2)}) collective-permute-start(bf16[1024,4096]{1,0:T(8,128)(2,1)} %get-tuple-element.56), channel_id=1, source_target_pairs={{0,1},{1,0},{2,3},{3,2},{4,5},{5,4},{6,7},{7,6}} | collective-permute-start | bytes 25165832 | tf_op jit(solution)/shard_map/ppermute | solution.py:46
  252.4 177.1 %collective-permute-start.14 = (bf16[1024,4096]{1,0:T(8,128)(2,1)}, bf16[1024,4096]{1,0:T(8,128)(2,1)}, u32[]{:S(2)}, u32[]{:S(2)}) collective-permute-start(bf16[1024,4096]{1,0:T(8,128)(2,1)} %get-tuple-element.54), channel_id=1, source_target_pairs={{0,1},{1,0},{2,3},{3,2},{4,5},{5,4},{6,7},{7,6}} | collective-permute-start | bytes 25165832 | tf_op jit(solution)/shard_map/ppermute | solution.py:46
  565.6 232.7 %collective-permute-start.30 = (bf16[4096,1024]{1,0:T(8,128)(2,1)}, bf16[4096,1024]{1,0:T(8,128)(2,1)}, u32[]{:S(2)}, u32[]{:S(2)}) collective-permute-start(bf16[4096,1024]{1,0:T(8,128)(2,1)} %get-tuple-element.34), channel_id=1, source_target_pairs={{0,1},{1,0},{2,3},{3,2},{4,5},{5,4},{6,7},{7,6}} | collective-permute-start | bytes 25165832 | tf_op jit(solution)/shard_map/ppermute | solution.py:46
  829.3 287.6 %collective-permute-start.43 = (f32[2048,512]{1,0:T(8,128)}, f32[2048,512]{1,0:T(8,128)}, u32[]{:S(2)}, u32[]{:S(2)}) collective-permute-start(f32[2048,512]{1,0:T(8,128)} %get-tuple-element.21), channel_id=1, source_target_pairs={{0,4},{4,0},{1,5},{5,1},{2,6},{6,2},{3,7},{7,3}} | collective-permute-start | bytes 12582920 | tf_op jit(solution)/shard_map/ppermute | solution.py:46
  894.3 208.5 %collective-permute-start.39 = (f32[2048,512]{1,0:T(8,128)}, f32[2048,512]{1,0:T(8,128)}, u32[]{:S(2)}, u32[]{:S(2)}) collective-permute-start(f32[2048,512]{1,0:T(8,128)} %get-tuple-element.19), channel_id=1, source_target_pairs={{0,4},{4,0},{1,5},{5,1},{2,6},{6,2},{3,7},{7,3}} | collective-permute-start | bytes 12582920 | tf_op jit(solution)/shard_map/ppermute | solution.py:46
  927.0 265.2 %collective-permute-start.47 = (f32[2048,512]{1,0:T(8,128)}, f32[2048,512]{1,0:T(8,128)}, u32[]{:S(2)}, u32[]{:S(2)}) collective-permute-start(f32[2048,512]{1,0:T(8,128)} %get-tuple-element.23), channel_id=1, source_target_pairs={{0,4},{4,0},{1,5},{5,1},{2,6},{6,2},{3,7},{7,3}} | collective-permute-start | bytes 12582920 | tf_op jit(solution)/shard_map/ppermute | solution.py:46
  1019.0 178.3 %collective-permute-start.36 = (f32[1024,512]{1,0:T(8,128)}, f32[1024,512]{1,0:T(8,128)S(1)}, u32[]{:S(2)}, u32[]{:S(2)}) collective-permute-start(f32[1024,512]{1,0:T(8,128)} %slice.298), channel_id=1, source_target_pairs={{0,2},{2,0},{1,3},{3,1},{4,6},{6,4},{5,7},{7,5}} | collective-permute-start | bytes 6291464 | tf_op jit(solution)/shard_map/ppermute | solution.py:46
  1268.1 201.3 %collective-permute-start.50 = (bf16[1024,1024]{1,0:T(8,128)(2,1)}, bf16[1024,1024]{1,0:T(8,128)(2,1)}, u32[]{:S(2)}, u32[]{:S(2)}) collective-permute-start(bf16[1024,1024]{1,0:T(8,128)(2,1)} %get-tuple-element.62), channel_id=1, source_target_pairs={{0,1},{1,0},{2,3},{3,2},{4,5},{5,4},{6,7},{7,6}} | collective-permute-start | bytes 6291464 | tf_op jit(solution)/shard_map/ppermute | solution.py:46
  1312.2 193.3 %collective-permute-start.53 = (bf16[1024,2048]{1,0:T(8,128)(2,1)}, bf16[1024,2048]{1,0:T(8,128)(2,1)}, u32[]{:S(2)}, u32[]{:S(2)}) collective-permute-start(bf16[1024,2048]{1,0:T(8,128)(2,1)} %multiply_convert_fusion), channel_id=1, source_target_pairs={{0,2},{2,0},{1,3},{3,1},{4,6},{6,4},{5,7},{7,5}} | collective-permute-start | bytes 12582920 | tf_op jit(solution)/shard_map/ppermute | solution.py:46
  1505.5 267.1 %collective-permute-start.54 = (bf16[1024,2048]{1,0:T(8,128)(2,1)}, bf16[1024,2048]{1,0:T(8,128)(2,1)}, u32[]{:S(2)}, u32[]{:S(2)}) collective-permute-start(bf16[1024,2048]{1,0:T(8,128)(2,1)} %collective-permute-done.53), channel_id=1, source_target_pairs={{0,4},{4,0},{1,5},{5,1},{2,6},{6,2},{3,7},{7,3}} | collective-permute-start | bytes 12582920 | tf_op jit(solution)/shard_map/ppermute | solution.py:46
  1547.4 179.8 %collective-permute-start.56 = (bf16[1024,1024]{1,0:T(8,128)(2,1)}, bf16[1024,1024]{1,0:T(8,128)(2,1)}, u32[]{:S(2)}, u32[]{:S(2)}) collective-permute-start(bf16[1024,1024]{1,0:T(8,128)(2,1)} %get-tuple-element.48), channel_id=1, source_target_pairs={{0,2},{2,0},{1,3},{3,1},{4,6},{6,4},{5,7},{7,5}} | collective-permute-start | bytes 6291464 | tf_op jit(solution)/shard_map/ppermute | solution.py:46
  1592.3 179.8 %collective-permute-start.59 = (bf16[1024,1024]{1,0:T(8,128)(2,1)}, bf16[1024,1024]{1,0:T(8,128)(2,1)}, u32[]{:S(2)}, u32[]{:S(2)}) collective-permute-start(bf16[1024,1024]{1,0:T(8,128)(2,1)} %get-tuple-element.41), channel_id=1, source_target_pairs={{0,2},{2,0},{1,3},{3,1},{4,6},{6,4},{5,7},{7,5}} | collective-permute-start | bytes 6291464 | tf_op jit(solution)/shard_map/ppermute | solution.py:46
  1638.4 178.5 %collective-permute-start.85 = (bf16[1024,1024]{1,0:T(8,128)(2,1)}, bf16[1024,1024]{1,0:T(8,128)(2,1)S(1)}, u32[]{:S(2)}, u32[]{:S(2)}) collective-permute-start(bf16[1024,1024]{1,0:T(8,128)(2,1)} %get-tuple-element.57), channel_id=1, source_target_pairs={{0,2},{2,0},{1,3},{3,1},{4,6},{6,4},{5,7},{7,5}} | collective-permute-start | bytes 6291464 | tf_op jit(solution)/shard_map/ppermute | solution.py:46
  1682.2 288.1 %collective-permute-start.55 = (bf16[1024,4096]{1,0:T(8,128)(2,1)}, bf16[1024,4096]{1,0:T(8,128)(2,1)}, u32[]{:S(2)}, u32[]{:S(2)}) collective-permute-start(bf16[1024,4096]{1,0:T(8,128)(2,1)} %get-tuple-element.55), channel_id=1, source_target_pairs={{0,1},{1,0},{2,3},{3,2},{4,5},{5,4},{6,7},{7,6}} | collective-permute-start | bytes 25165832 | tf_op jit(solution)/shard_map/ppermute | solution.py:46
  1727.1 243.5 %collective-permute-start.58 = (bf16[1024,4096]{1,0:T(8,128)(2,1)}, bf16[1024,4096]{1,0:T(8,128)(2,1)}, u32[]{:S(2)}, u32[]{:S(2)}) collective-permute-start(bf16[1024,4096]{1,0:T(8,128)(2,1)} %get-tuple-element.53), channel_id=1, source_target_pairs={{0,1},{1,0},{2,3},{3,2},{4,5},{5,4},{6,7},{7,6}} | collective-permute-start | bytes 25165832 | tf_op jit(solution)/shard_map/ppermute | solution.py:46
  1874.8 183.7 %collective-permute-start.90 = (bf16[4096,1024]{1,0:T(8,128)(2,1)}, bf16[4096,1024]{1,0:T(8,128)(2,1)}, u32[]{:S(2)}, u32[]{:S(2)}) collective-permute-start(bf16[4096,1024]{1,0:T(8,128)(2,1)} %get-tuple-element.33), channel_id=1, source_target_pairs={{0,4},{4,0},{1,5},{5,1},{2,6},{6,2},{3,7},{7,3}} | collective-permute-start | bytes 25165832 | tf_op jit(solution)/shard_map/ppermute | solution.py:46
  2017.0 184.6 %collective-permute-start.84 = (bf16[4096,1024]{1,0:T(8,128)(2,1)}, bf16[4096,1024]{1,0:T(8,128)(2,1)}, u32[]{:S(2)}, u32[]{:S(2)}) collective-permute-start(bf16[4096,1024]{1,0:T(8,128)(2,1)} %get-tuple-element.33), channel_id=1, source_target_pairs={{0,1},{1,0},{2,3},{3,2},{4,5},{5,4},{6,7},{7,6}} | collective-permute-start | bytes 25165832 | tf_op jit(solution)/shard_map/ppermute | solution.py:46
  2199.5 226.9 %collective-permute-start.80 = (bf16[2,512,1024]{2,1,0:T(8,128)(2,1)}, bf16[2,512,1024]{2,1,0:T(8,128)(2,1)S(1)}, u32[]{:S(2)}, u32[]{:S(2)}) collective-permute-start(bf16[2,512,1024]{2,1,0:T(8,128)(2,1)} %dynamic-slice_bitcast_fusion.12), channel_id=1, source_target_pairs={{0,4},{4,0},{1,5},{5,1},{2,6},{6,2},{3,7},{7,3}} | collective-permute-start | bytes 6291464 | tf_op jit(solution)/shard_map/ppermute | solution.py:46
  2200.1 226.3 %collective-permute-start.79 = (bf16[2,512,1024]{2,1,0:T(8,128)(2,1)}, bf16[2,512,1024]{2,1,0:T(8,128)(2,1)}, u32[]{:S(2)}, u32[]{:S(2)}) collective-permute-start(bf16[2,512,1024]{2,1,0:T(8,128)(2,1)} %dynamic-slice_bitcast_fusion.13), channel_id=1, source_target_pairs={{0,4},{4,0},{1,5},{5,1},{2,6},{6,2},{3,7},{7,3}} | collective-permute-start | bytes 6291464 | tf_op jit(solution)/shard_map/ppermute | solution.py:46
  2201.6 225.4 %collective-permute-start.78 = (bf16[2,512,1024]{2,1,0:T(8,128)(2,1)}, bf16[2,512,1024]{2,1,0:T(8,128)(2,1)}, u32[]{:S(2)}, u32[]{:S(2)}) collective-permute-start(bf16[2,512,1024]{2,1,0:T(8,128)(2,1)} %dynamic-slice_bitcast_fusion.14), channel_id=1, source_target_pairs={{0,4},{4,0},{1,5},{5,1},{2,6},{6,2},{3,7},{7,3}} | collective-permute-start | bytes 6291464 | tf_op jit(solution)/shard_map/ppermute | solution.py:46
  2202.2 225.8 %collective-permute-start.77 = (bf16[2,512,1024]{2,1,0:T(8,128)(2,1)}, bf16[2,512,1024]{2,1,0:T(8,128)(2,1)}, u32[]{:S(2)}, u32[]{:S(2)}) collective-permute-start(bf16[2,512,1024]{2,1,0:T(8,128)(2,1)} %dynamic-slice_bitcast_fusion.15), channel_id=1, source_target_pairs={{0,4},{4,0},{1,5},{5,1},{2,6},{6,2},{3,7},{7,3}} | collective-permute-start | bytes 6291464 | tf_op jit(solution)/shard_map/ppermute | solution.py:46
  2232.4 192.6 %collective-permute-start.81 = (bf16[2,512,512]{2,1,0:T(8,128)(2,1)S(1)}, bf16[2,512,512]{2,1,0:T(8,128)(2,1)S(1)}, u32[]{:S(2)}, u32[]{:S(2)}) collective-permute-start(bf16[2,512,512]{2,1,0:T(8,128)(2,1)S(1)} %dynamic-slice_bitcast_fusion.41), channel_id=1, source_target_pairs={{0,4},{4,0},{1,5},{5,1},{2,6},{6,2},{3,7},{7,3}} | collective-permute-start | bytes 3145736 | tf_op jit(solution)/shard_map/ppermute | solution.py:46
  (168 other events, 9653.6 us)
